TPU v7x, 256 devices: a whole 4x4x8 slice. The times are simulated.
256 devices in a mesh: gx: 16 (over y_lo, z), gy: 16 (over x, y_hi, core).
Axes of the slice: x: 4, y: 4 (y_hi: 2, y_lo: 2; y = y_hi * 2 + y_lo), z: 8, core: 2. Of those that a mesh axis runs over, the one named last changes fastest.
Arguments:
- modes: float32 [2, 3, 192, 256, 128], P(None, None, 'gx', 'gy'), may hold values from -6 to 6
- moduli: float32 [192, 256, 128], P('gx', 'gy'), may hold values from 0.5 to 2
- pinned: int32 [192, 256, 128], P('gx', 'gy'), may hold values 0 or 1
- spectrum: float32 [3, 2], replicated, may hold values from 0.175 to 5, as said below
Outputs:
- correction: float32 [2, 3, 192, 256, 128], P(None, None, 'gx', 'gy')
Inputs may be any that keep to these rules, and one draw needn't show every extreme that they name: spectrum[l] = (lower, upper) with upper from 3.5 to 5 and lower 0.05 to 0.15 times upper.
All inputs are finite; a program needn't handle non-finite values. No bound on the sum of `pinned` on one device may be relied on, other than what follows from the above.
Results may differ from a plain program's by a relative error of at most 0.0003.
Values sent between devices are 32-bit elements; how exact they have to be, the bound alone decides.
A program may use at most 128 MiB of HBM per device.

v0:
```python
import functools

import jax
import jax.numpy as jnp
import ml_dtypes
import numpy as np
from jax import lax
from jax.experimental import pallas as pl
from jax.experimental.pallas import tpu as pltpu
from jax.sharding import PartitionSpec as P

MESH = pl.DeviceIdType.MESH
BF = jnp.bfloat16
F32 = jnp.float32

MU_SHEAR = 1.0
LAMBDA_BULK = 1.5
CROSS = MU_SHEAR + LAMBDA_BULK
VECS = 2
EX, EY = 3, 4
DEGREES = (4, 2, 1)
ROWS = (224, 64, 32)
KPAD = (256, 128, 128)
LANES = (256, 128, 128)
STEPS = (3, 3, 4)

PROLONG = {
    4: np.array([[1.0, 0.0, 0.0], [0.375, 0.75, -0.125], [0.0, 1.0, 0.0], [-0.125, 0.75, 0.375]]),
    2: np.array([[1.0, 0.0], [0.5, 0.5]]),
}

DIRS = ((-1, 0), (1, 0), (0, -1), (0, 1), (-1, -1), (1, 1), (1, -1), (-1, 1))


def element_matrices(degree):
    points, weights = np.polynomial.legendre.leggauss(8)
    points, weights = 0.5 * (points + 1.0), 0.5 * weights
    nodes = np.arange(degree + 1) / degree
    values = np.zeros((degree + 1, 8))
    slopes = np.zeros((degree + 1, 8))
    for i in range(degree + 1):
        others = [j for j in range(degree + 1) if j != i]
        values[i] = np.prod([(points - nodes[j]) / (nodes[i] - nodes[j]) for j in others], axis=0)
        for skip in others:
            part = np.ones(8) / (nodes[i] - nodes[skip])
            for j in others:
                if j != skip:
                    part = part * (points - nodes[j]) / (nodes[i] - nodes[j])
            slopes[i] += part
    mass = (values * weights) @ values.T
    stiff = (slopes * weights) @ slopes.T
    mixed = (slopes * weights) @ values.T
    return [mass, stiff, mixed, mixed.T]


def assembled(element, count, first):
    degree = element.shape[0] - 1
    full = np.zeros((count * degree + 1, count * degree + 1))
    for e in range(count):
        full[e * degree : (e + 1) * degree + 1, e * degree : (e + 1) * degree + 1] += element
    if first:
        full[0, 0] += element[degree, degree]
    return full


def node_rows(degree):
    px, py = EX * degree, EY * degree
    rows = [(x, y) for x in range(px) for y in range(py)]
    rows += [(px, y) for y in range(py + 1)]
    rows += [(x, py) for x in range(px)]
    return rows


def split(values, terms):
    out, rest = [], np.asarray(values, np.float32)
    for _ in range(terms):
        part = rest.astype(ml_dtypes.bfloat16)
        out.append(part)
        rest = rest - part.astype(np.float32)
    return out


def interpolation(degree, elements, closed):
    table = PROLONG[degree]
    half = degree // 2
    full = np.zeros((elements * degree + 1, elements * half + 1))
    for e in range(elements):
        for a in range(degree):
            for t in range(table.shape[1]):
                full[e * degree + a, e * half + t] += table[a, t]
    full[elements * degree, elements * half] = 1.0
    return full if closed else full[:-1, :-1]


def constants(z_nodes):
    out = {}
    elements_z = z_nodes // 4
    for level, degree in enumerate(DEGREES):
        n, kpad, lanes = ROWS[level], KPAD[level], LANES[level]
        rows = node_rows(degree)
        mats = element_matrices(degree)
        nz = elements_z * degree
        pick_x = np.zeros((n, 16), np.float32)
        pick_y = np.zeros((n, 32), np.float32)
        for r, (x, y) in enumerate(rows):
            pick_x[r, x] = 1.0
            pick_y[r, y] = 1.0
        out["rx", level] = np.concatenate([pick_x] * 3, 1).astype(ml_dtypes.bfloat16)
        out["ry", level] = np.concatenate([pick_y] * 3, 1).astype(ml_dtypes.bfloat16)
        tx = np.zeros((2, 4, 48, kpad), ml_dtypes.bfloat16)
        ty = np.zeros((2, 4, 96, kpad), ml_dtypes.bfloat16)
        for first in range(2):
            for op in range(4):
                ex = assembled(mats[op], EX, first)
                ey = assembled(mats[op], EY, first)
                wide_x = np.zeros((16, kpad))
                wide_y = np.zeros((32, kpad))
                for c, (x, y) in enumerate(rows):
                    wide_x[: ex.shape[0], c] = ex[:, x]
                    wide_y[: ey.shape[0], c] = ey[:, y]
                tx[first, op] = np.concatenate(split(wide_x, 3), 0)
                ty[first, op] = np.concatenate(split(wide_y, 3), 0)
        out["tx", level], out["ty", level] = tx, ty
        copies = 1 if nz >= 128 else VECS
        zmats = []
        for op in range(4):
            ez = assembled(mats[op], elements_z, True)[:nz, :nz].T
            block = np.zeros((128, 128))
            for v in range(copies):
                block[v * nz : (v + 1) * nz, v * nz : (v + 1) * nz] = ez
            zmats.append(block)
        stacks = []
        for third in (2, 3):
            wide = np.concatenate([zmats[0], zmats[1], zmats[third]], 1)
            hi, lo = split(wide, 2)
            stacks.append(np.concatenate([hi, hi, lo], 0))
        out["z", level] = np.stack(stacks)
        weights = MU_SHEAR + CROSS * np.eye(3)

        def center(op, count):
            full = assembled(mats[op], count, True)
            diag = np.array([full[i % degree, i % degree] for i in range(count * degree)])
            diag[::degree] = mats[op][0, 0] + mats[op][degree, degree]
            return np.append(diag, diag[0])

        cx = [center(op, EX) for op in (0, 1)]
        cy = [center(op, EY) for op in (0, 1)]
        cz = [center(op, elements_z)[:nz] for op in (0, 1)]
        kd = np.ones((3, n, 128), np.float32)
        for c in range(3):
            for r, (x, y) in enumerate(rows):
                row = (
                    weights[c, 0] * cx[1][x] * cy[0][y] * cz[0]
                    + weights[c, 1] * cx[0][x] * cy[1][y] * cz[0]
                    + weights[c, 2] * cx[0][x] * cy[0][y] * cz[1]
                )
                kd[c, r, : copies * nz] = np.tile(row, copies)
        out["kd", level] = kd
        if level == 2:
            continue
        half = DEGREES[level + 1]
        nzc = elements_z * half
        coarse_rows = node_rows(half)
        px_, py_ = interpolation(degree, EX, True), interpolation(degree, EY, True)
        pz_ = interpolation(degree, elements_z, False)
        pxy = np.zeros((n, 128), np.float32)
        sample = np.zeros((ROWS[level + 1], kpad), np.float32)
        for c, (xc, yc) in enumerate(coarse_rows):
            for r, (x, y) in enumerate(rows):
                pxy[r, c] = px_[x, xc] * py_[y, yc]
            sample[c, rows.index((2 * xc, 2 * yc))] = 1.0
        rxy = np.zeros((ROWS[level + 1], kpad), np.float32)
        rxy[:, :n] = pxy[:, : ROWS[level + 1]].T
        pz = np.zeros((128, lanes), np.float32)
        for v in range(VECS):
            pz[v * nzc : (v + 1) * nzc, v * nz : (v + 1) * nz] = pz_.T
        sample_z = np.zeros((128, 128), np.float32)
        for v in range(VECS):
            for z in range(nzc):
                sample_z[2 * z, v * nzc + z] = 1.0
        for name, value in (
            ("pxy", pxy),
            ("rxy", rxy),
            ("pz", np.concatenate([pz, pz], 0)),
            ("rz", np.concatenate([pz.T, pz.T], 0)),
            ("sxy", sample),
            ("sz", sample_z),
        ):
            rounded = value.astype(ml_dtypes.bfloat16)
            assert (rounded.astype(np.float32) == value).all()
            out[name, level] = rounded
    return out


M_, K_, G_, T_ = range(4)
SLOT_OF = {(0, K_): 0, (0, M_): 1, (1, M_): 2, (2, T_): 3, (1, K_): 4, (2, M_): 5, (2, K_): 6, (0, G_): 7, (1, G_): 8}
FIRST_SLOT = (0, 1, 5)
ON = MU_SHEAR + CROSS
BLOCKS = (
    (((MU_SHEAR, M_, M_),), ((ON, K_, M_), (MU_SHEAR, M_, K_)), ((CROSS, G_, T_),), ((CROSS, G_, M_),)),
    (((CROSS, T_, G_),), ((MU_SHEAR, K_, M_), (ON, M_, K_)), ((CROSS, M_, G_),), ((MU_SHEAR, M_, M_),)),
    (((MU_SHEAR, K_, M_), (MU_SHEAR, M_, K_)), ((ON, M_, M_),), ((CROSS, T_, M_),), ((CROSS, M_, T_),)),
)


def rounded8(value):
    return (value + 7) // 8 * 8


def dot(a, b):
    return jnp.dot(a, b, preferred_element_type=F32)


def halves(value):
    hi = value.astype(BF)
    return hi, (value - hi.astype(F32)).astype(BF)


def kernel(size_x, size_y, names, *refs):
    modes, moduli, pinned, spectrum = refs[:4]
    const_hbm = dict(zip(names, refs[4 : 4 + len(names)]))
    at = 4 + len(names)
    out = refs[at]
    scratch = dict(zip(SCRATCH_NAMES(names), refs[at + 1 :]))
    const = {name: scratch["const", name] for name in names}
    load_sem, send_sems, recv_sems = scratch["load"], scratch["send"], scratch["recv"]
    first_send, first_recv = scratch["first_send"], scratch["first_recv"]

    ix, iy = lax.axis_index("gx"), lax.axis_index("gy")

    def exists(dx, dy):
        jx, jy = ix + dx, iy + dy
        return (jx >= 0) & (jx < size_x) & (jy >= 0) & (jy < size_y)

    loads = []

    def load(src, dst):
        copy = pltpu.make_async_copy(src, dst, load_sem.at[len(loads)])
        copy.start()
        loads.append(copy)

    state = lambda name, level: scratch[name, level]
    b0 = state("b", 0)
    own0 = EX * 4 * EY * 4
    for v in range(VECS):
        for c in range(3):
            load(modes.at[v, c], b0.at[c, 0:own0, v * 128 : (v + 1) * 128])
    load(moduli, scratch["w"])
    load(pinned, scratch["pin"])
    n_first = len(loads)
    edge_x = jnp.where(ix == 0, 1, 0)
    edge_y = jnp.where(iy == 0, 1, 0)
    for name in names:
        if name[0] == "tx":
            load(const_hbm[name].at[edge_x], const[name])
        elif name[0] == "ty":
            load(const_hbm[name].at[edge_y], const[name])
        else:
            load(const_hbm[name], const[name])

    for level in range(3):
        for name in ("recv_x", "recv_y", "recv_c"):
            ref = scratch[name, level]
            ref[...] = jnp.zeros_like(ref)
    for name in ("first_x", "first_y", "first_c"):
        scratch[name][...] = jnp.zeros_like(scratch[name])

    barrier = pltpu.get_barrier_semaphore()
    count = jnp.int32(0)
    for dx, dy in DIRS:
        here = exists(dx, dy)
        count = count + jnp.where(here, 1, 0)

        @pl.when(here)
        def _():
            pl.semaphore_signal(barrier, inc=1, device_id=(ix + dx, iy + dy), device_id_type=MESH)

    for level in range(3):
        for name in ("send_x", "send_y", "send_c"):
            ref = state(name, level)
            ref[...] = jnp.zeros_like(ref)
        ref = state("zhi", level)
        ref[...] = jnp.zeros_like(ref)
        ref = state("zlo", level)
        ref[...] = jnp.zeros_like(ref)
    for name in ("tmp_hi", "tmp_mid", "tmp_lo"):
        scratch[name][...] = jnp.zeros_like(scratch[name])
    b0[:, own0:, :] = jnp.zeros((3, ROWS[0] - own0, 256), F32)
    m0, s0 = state("m", 0), state("s", 0)
    m0[own0:, :] = jnp.zeros((ROWS[0] - own0, 128), F32)
    s0[own0:, :] = jnp.zeros((ROWS[0] - own0, 128), F32)

    for copy in loads[:n_first]:
        copy.wait()

    m0[0:own0, :] = 1.0 - scratch["pin"][...].astype(F32)
    s0[0:own0, :] = scratch["w"][...] * m0[0:own0, :]

    fx, fy, fc = scratch["first_out_x"], scratch["first_out_y"], scratch["first_out_c"]
    fc[...] = jnp.zeros_like(fc)
    for c in range(3):
        fx[16 * c : 16 * c + 16, :] = b0[c, 0:16, :]
        for x in range(12):
            fy[12 * c + x : 12 * c + x + 1, :] = b0[c, 16 * x : 16 * x + 1, :]
        fc[c : c + 1, :] = b0[c, 0:1, :]
    for k, ref in enumerate((s0, m0)):
        lane = slice(128 * k, 128 * k + 128)
        fx[48:64, lane] = ref[0:16, :]
        for x in range(12):
            fy[36 + x : 37 + x, lane] = ref[16 * x : 16 * x + 1, :]
        fc[3:4, lane] = ref[0:1, :]

    pl.semaphore_wait(barrier, count)

    first = (
        (fx, scratch["first_x"], (-1, 0)),
        (fy, scratch["first_y"], (0, -1)),
        (fc, scratch["first_c"], (-1, -1)),
    )

    def first_copy(k):
        src, dst, (dx, dy) = first[k]
        return pltpu.make_async_remote_copy(
            src_ref=src,
            dst_ref=dst,
            send_sem=first_send.at[k],
            recv_sem=first_recv.at[k],
            device_id=(ix + dx, iy + dy),
            device_id_type=MESH,
        )

    for k in range(3):
        dx, dy = first[k][2]

        @pl.when(exists(dx, dy))
        def _():
            first_copy(k).start()

    coef = scratch["coef"]
    for level in range(3):
        low = jnp.full((1, 256), spectrum[level, 0], F32)
        top = jnp.full((1, 256), spectrum[level, 1], F32)
        center, radius = 0.5 * (top + low), 0.5 * (top - low)
        sigma = center / radius
        rho = 1.0 / sigma
        coef[level * 8] = jnp.zeros((1, 256), F32)
        coef[level * 8 + 1] = 1.0 / center
        for i in range(1, STEPS[level]):
            rho_next = 1.0 / (2.0 * sigma - rho)
            coef[level * 8 + 2 * i] = rho_next * rho
            coef[level * 8 + 2 * i + 1] = 2.0 * rho_next / radius
            rho = rho_next

    for copy in loads[n_first:]:
        copy.wait()

    for level in range(3):
        kpad = KPAD[level]
        xe, ye = state("xe", level), state("ye", level)
        for op in range(4):
            xe[op] = dot(const["rx", level][...], const["tx", level][op])
            ye[op] = dot(const["ry", level][...], const["ty", level][op])
        ahi, alo = state("ahi", level), state("alo", level)
        for c in range(3):
            for j in range(4):
                value = None
                for factor, xop, yop in BLOCKS[c][j]:
                    term = xe[xop] * ye[yop]
                    if factor != 1.0:
                        term = factor * term
                    value = term if value is None else value + term
                hi, lo = halves(value)
                ahi[c, :, j * kpad : (j + 1) * kpad] = hi
                alo[c, :, j * kpad : (j + 1) * kpad] = lo

    for k in range(3):
        dx, dy = first[k][2]

        @pl.when(exists(-dx, -dy))
        def _():
            first_copy(k).wait_recv()

        @pl.when(exists(dx, dy))
        def _():
            first_copy(k).wait_send()

    gx_, gy_, gc_ = scratch["first_x"], scratch["first_y"], scratch["first_c"]
    for c in range(3):
        b0[c, 192:208, :] = gx_[16 * c : 16 * c + 16, :]
        b0[c, 208:209, :] = gc_[c : c + 1, :]
        b0[c, 209:221, :] = gy_[12 * c : 12 * c + 12, :]
    for k, ref in enumerate((s0, m0)):
        lane = slice(128 * k, 128 * k + 128)
        ref[192:208, :] = gx_[48:64, lane]
        ref[208:209, :] = gc_[3:4, lane]
        ref[209:221, :] = gy_[36:48, lane]

    for level in range(2):
        kpad = KPAD[level]
        n = ROWS[level]
        for name in ("s", "m"):
            rest = state(name, level)[...]
            total = None
            for term in range(1 if name == "m" else 3):
                part = rest.astype(BF)
                rest = rest - part.astype(F32)
                scratch["tmp_hi"][0:n, :] = dot(part, const["sz", level][...]).astype(BF)
                got = dot(const["sxy", level][...], scratch["tmp_hi"][0:kpad, :])
                total = got if total is None else total + got
            state(name, level + 1)[...] = total

    def wide(value, level):
        return jnp.concatenate([value, value], 1) if LANES[level] == 256 else value

    for level in range(3):
        s, m = state("s", level)[...], state("m", level)[...]
        for c in range(3):
            state("dinv", level)[c] = 1.0 / (s * s * const["kd", level][c] + (1.0 - m))

    def apply_partial(level, source, target):
        n, kpad, lanes = ROWS[level], KPAD[level], LANES[level]
        zhi, zlo = state("zhi", level), state("zlo", level)
        s = state("s", level)[...]
        for c in range(3):
            ops = (M_, K_, T_ if c == 2 else G_)
            for h in range(lanes // 128):
                lane = slice(128 * h, 128 * h + 128)
                hi, lo = halves(s * source[c, :, lane])
                prod = dot(jnp.concatenate([hi, lo, hi], 1), const["z", level][1 if c == 2 else 0])
                for k, op in enumerate(ops):
                    slot = SLOT_OF[c, op]
                    zh, zl = halves(prod[:, 128 * k : 128 * k + 128])
                    zhi[slot * kpad : slot * kpad + n, lane] = zh
                    zlo[slot * kpad : slot * kpad + n, lane] = zl
        ahi, alo = state("ahi", level), state("alo", level)
        for c in range(3):
            span = slice(FIRST_SLOT[c] * kpad, (FIRST_SLOT[c] + 4) * kpad)
            value = dot(ahi[c], zhi[span, :]) + dot(ahi[c], zlo[span, :]) + dot(alo[c], zhi[span, :])
            target[c] = value

    def exchange(level, slot, t):
        p = DEGREES[level]
        px, py = EX * p, EY * p
        nown = px * py
        nx, ny = py + 1, px + 1
        sx, sy, sc = state("send_x", level), state("send_y", level), state("send_c", level)
        rx, ry, rc = state("recv_x", level), state("recv_y", level), state("recv_c", level)
        corner = nown + py
        for c in range(3):
            sx[slot, 0, c * nx : c * nx + py, :] = t[c, 0:py, :]
            sx[slot, 0, c * nx + py : c * nx + nx, :] = t[c, corner + 1 : corner + 2, :]
            sx[slot, 1, c * nx : c * nx + nx, :] = t[c, nown : nown + nx, :]
            sy[slot, 0, c * ny : c * ny + 1, :] = t[c, nown : nown + 1, :]
            for x in range(px):
                sy[slot, 0, c * ny + 1 + x : c * ny + 2 + x, :] = t[c, x * py : x * py + 1, :]
            sy[slot, 1, c * ny : c * ny + ny, :] = t[c, corner : corner + ny, :]
            for k, row in enumerate((0, corner, nown, corner + 1)):
                sc[slot, k, c : c + 1, :] = t[c, row : row + 1, :]

        def copy(d):
            dx, dy = DIRS[d]
            src, dst, k = ((sx, rx, d), (sy, ry, d - 2), (sc, rc, d - 4))[0 if d < 2 else 1 if d < 4 else 2]
            return pltpu.make_async_remote_copy(
                src_ref=src.at[slot, k],
                dst_ref=dst.at[slot, k],
                send_sem=send_sems.at[level, slot, d],
                recv_sem=recv_sems.at[level, slot, d],
                device_id=(ix + dx, iy + dy),
                device_id_type=MESH,
            )

        for d in (2, 3, 4, 5, 6, 7, 0, 1):

            @pl.when(exists(*DIRS[d]))
            def _():
                copy(d).start()

        for d in range(8):
            dx, dy = DIRS[d]

            @pl.when(exists(-dx, -dy))
            def _():
                copy(d).wait_recv()

        for c in range(3):
            t[c, nown : nown + nx, :] += rx[slot, 0, c * nx : c * nx + nx, :]
            t[c, 0:py, :] += rx[slot, 1, c * nx : c * nx + py, :]
            t[c, corner + 1 : corner + 2, :] += rx[slot, 1, c * nx + py : c * nx + nx, :]
            t[c, corner : corner + ny, :] += ry[slot, 0, c * ny : c * ny + ny, :]
            t[c, nown : nown + 1, :] += ry[slot, 1, c * ny : c * ny + 1, :]
            for x in range(px):
                t[c, x * py : x * py + 1, :] += ry[slot, 1, c * ny + 1 + x : c * ny + 2 + x, :]
            for k, row in enumerate((corner, 0, corner + 1, nown)):
                t[c, row : row + 1, :] += rc[slot, k, c : c + 1, :]

        for d in range(8):

            @pl.when(exists(*DIRS[d]))
            def _():
                copy(d).wait_send()

    def step(level, i, slot):
        r, d, x, t = (state(name, level) for name in ("r", "d", "x", "t"))
        apply_partial(level, d, t)
        exchange(level, slot, t)
        s = wide(state("s", level)[...], level)
        f = 1.0 - wide(state("m", level)[...], level)
        lanes = LANES[level]
        alpha = coef[level * 8 + 2 * i][:, :lanes]
        beta = coef[level * 8 + 2 * i + 1][:, :lanes]
        for c in range(3):
            old = d[c]
            res = r[c] - (s * t[c] + f * old)
            r[c] = res
            new = alpha * old + beta * (wide(state("dinv", level)[c], level) * res)
            d[c] = new
            x[c] = x[c] + new

    def start(level):
        b, r, d, x = (state(name, level) for name in ("b", "r", "d", "x"))
        beta = coef[level * 8 + 1][:, : LANES[level]]
        for c in range(3):
            res = b[c]
            new = beta * (wide(state("dinv", level)[c], level) * res)
            r[c] = res
            d[c] = new
            x[c] = new

    def restart(level):
        b, r, d, x = (state(name, level) for name in ("b", "r", "d", "x"))
        r[...] = b[...]
        d[...] = x[...]

    def restrict(level, slot):
        n, n_next = ROWS[level], ROWS[level + 1]
        x, t, b = state("x", level), state("t", level), state("b", level)
        apply_partial(level, x, t)
        p = DEGREES[level]
        nown = EX * p * EY * p
        s = wide(state("s", level)[...], level)
        m = wide(state("m", level)[...], level)
        rows = lax.broadcasted_iota(jnp.int32, (n, LANES[level]), 0)
        m = jnp.where(rows < nown, m, 0.0)
        t_next = state("t", level + 1)
        hi_ref, lo_ref = scratch["tmp_hi"], scratch["tmp_lo"]
        for c in range(3):
            y = m * b[c] - s * t[c]
            hi, lo = halves(y)
            yz = dot(jnp.concatenate([hi, lo], 1), const["rz", level][...])
            hi, lo = halves(yz)
            hi_ref[0:n, :] = hi
            lo_ref[0:n, :] = lo
            mat = const["rxy", level][...]
            t_next[c] = dot(mat, hi_ref[0 : KPAD[level], :]) + dot(mat, lo_ref[0 : KPAD[level], :])
        exchange(level + 1, slot, t_next)
        m_next = state("m", level + 1)[...]
        for c in range(3):
            state("b", level + 1)[c] = m_next * t_next[c]

    def prolong(level):
        n_next, lanes = ROWS[level + 1], LANES[level]
        e, x = state("x", level + 1), state("x", level)
        m = wide(state("m", level)[...], level)
        hi_ref, lo_ref = scratch["wide_hi"], scratch["wide_lo"]
        for c in range(3):
            hi, lo = halves(e[c])
            ez = dot(jnp.concatenate([hi, lo], 1), const["pz", level][...])
            hi, lo = halves(ez)
            hi_ref[0:n_next, 0:lanes] = hi
            lo_ref[0:n_next, 0:lanes] = lo
            mat = const["pxy", level][...]
            fine = dot(mat, hi_ref[:, 0:lanes]) + dot(mat, lo_ref[:, 0:lanes])
            x[c] = x[c] + m * fine

    for name in ("wide_hi", "wide_lo"):
        scratch[name][...] = jnp.zeros_like(scratch[name])

    def steps(level, begin, end, first_exchange):
        def body(i, carry):
            step(level, i, lax.rem(first_exchange + i - begin, 2))
            return carry

        lax.fori_loop(begin, end, body, 0)

    start(0)
    steps(0, 1, 3, 0)
    restrict(0, 0)
    start(1)
    steps(1, 1, 3, 1)
    restrict(1, 0)
    start(2)
    steps(2, 1, 4, 1)
    prolong(1)
    restart(1)
    steps(1, 0, 3, 3)
    prolong(0)
    restart(0)
    steps(0, 0, 3, 2)

    x0 = state("x", 0)
    stores = []
    for v in range(VECS):
        for c in range(3):
            copy = pltpu.make_async_copy(
                x0.at[c, 0:own0, v * 128 : (v + 1) * 128], out.at[v, c], load_sem.at[v * 3 + c]
            )
            copy.start()
            stores.append(copy)
    for copy in stores:
        copy.wait()


def scratch_list(names, shapes):
    items = []
    for name in names:
        shape, dtype = shapes[name]
        if name[0] in ("tx", "ty"):
            shape = shape[1:]
        items.append((("const", name), pltpu.VMEM(shape, dtype)))
    for level in range(3):
        n, kpad, lanes = ROWS[level], KPAD[level], LANES[level]
        for name in ("b", "r", "d", "x", "t"):
            items.append(((name, level), pltpu.VMEM((3, n, lanes), F32)))
        items.append((("dinv", level), pltpu.VMEM((3, n, 128), F32)))
        for name in ("s", "m"):
            items.append(((name, level), pltpu.VMEM((n, 128), F32)))
        for name in ("xe", "ye"):
            items.append(((name, level), pltpu.VMEM((4, n, kpad), F32)))
        for name in ("ahi", "alo"):
            items.append(((name, level), pltpu.VMEM((3, n, 4 * kpad), BF)))
        for name in ("zhi", "zlo"):
            items.append(((name, level), pltpu.VMEM((9 * kpad, lanes), BF)))
        nx, ny = rounded8(3 * (EY * DEGREES[level] + 1)), rounded8(3 * (EX * DEGREES[level] + 1))
        for name in ("send", "recv"):
            items.append(((name + "_x", level), pltpu.VMEM((2, 2, nx, lanes), F32)))
            items.append(((name + "_y", level), pltpu.VMEM((2, 2, ny, lanes), F32)))
            items.append(((name + "_c", level), pltpu.VMEM((2, 4, 8, lanes), F32)))
    for name in ("first_out", "first"):
        items.append((name + "_x", pltpu.VMEM((64, 256), F32)))
        items.append((name + "_y", pltpu.VMEM((48, 256), F32)))
        items.append((name + "_c", pltpu.VMEM((8, 256), F32)))
    for name in ("tmp_hi", "tmp_mid", "tmp_lo"):
        items.append((name, pltpu.VMEM((256, 128), BF)))
    for name in ("wide_hi", "wide_lo"):
        items.append((name, pltpu.VMEM((128, 256), BF)))
    items.append(("w", pltpu.VMEM((EX * 4 * EY * 4, 128), F32)))
    items.append(("pin", pltpu.VMEM((EX * 4 * EY * 4, 128), jnp.int32)))
    items.append(("coef", pltpu.VMEM((24, 1, 256), F32)))
    items.append(("load", pltpu.SemaphoreType.DMA((8 + len(names),))))
    items.append(("send", pltpu.SemaphoreType.DMA((3, 2, 8))))
    items.append(("recv", pltpu.SemaphoreType.DMA((3, 2, 8))))
    items.append(("first_send", pltpu.SemaphoreType.DMA((3,))))
    items.append(("first_recv", pltpu.SemaphoreType.DMA((3,))))
    return items


def SCRATCH_NAMES(names):
    shapes = {name: ((1, 1), BF) for name in names}
    return [name for name, _ in scratch_list(names, shapes)]


def solution(mesh):
    size_x, size_y = mesh.shape["gx"], mesh.shape["gy"]
    tables = constants(128)
    names = tuple(tables)
    shapes = {name: (tables[name].shape, tables[name].dtype) for name in names}

    def local(modes, moduli, pinned, spectrum):
        own = modes.shape[2] * modes.shape[3]
        any_spec = pl.BlockSpec(memory_space=pl.ANY)
        out = pl.pallas_call(
            functools.partial(kernel, size_x, size_y, names),
            out_shape=jax.ShapeDtypeStruct((VECS, 3, own, 128), F32),
            in_specs=[any_spec] * 3 + [pl.BlockSpec(memory_space=pltpu.SMEM)] + [any_spec] * len(names),
            out_specs=any_spec,
            scratch_shapes=[item for _, item in scratch_list(names, shapes)],
            compiler_params=pltpu.CompilerParams(
                collective_id=0, has_side_effects=True, vmem_limit_bytes=60 * 1024 * 1024
            ),
        )(
            modes.reshape(VECS, 3, own, 128),
            moduli.reshape(own, 128),
            pinned.reshape(own, 128),
            spectrum,
            *[jnp.asarray(tables[name]) for name in names],
        )
        return out.reshape(modes.shape)

    return jax.shard_map(
        local,
        mesh=mesh,
        in_specs=(P(None, None, "gx", "gy", None), P("gx", "gy", None), P("gx", "gy", None), P()),
        out_specs=P(None, None, "gx", "gy", None),
        check_vma=False,
    )
```

profile of v0, /device:TPU:25, one launch (start us, length us, event | category | flops | bytes accessed | tf_op | source)
XLA Modules:
  0.0 109.3 jit_solution(16792028548443760172)
XLA Ops:
  0.0 0.0 copy-start
  0.0 0.7 copy-done
  0.7 0.7 copy.35.refs_3_
  1.3 106.0 %shard_map.316 = f32[2,3,192,128]{3,2,1,0:T(8,128)} custom-call(f32[2,3,192,128]{3,2,1,0:T(8,128)} %bitcast.5, f32[192,128]{1,0:T(8,128)} %bitcast.6, s32[192,128]{1,0:T(8,128)} %bitcast.7, f32[3,2]{1,0:T(4,128)} %copy.35.refs_3_, bf16[224,48]{1,0:T(8,128)(2,1)} %constant.60.clone.refs_4_, bf16[224,96]{1,0:T(8,128)(2,1)} %constant.61.clone.refs_5_, ...), custom_call_target="tpu_custom_call" | custom-call | tf_op jit(solution)/shard_map/pallas_call | solution.py:671
  107.4 1.9 %copy.37 = f32[2,3,12,16,128]{4,3,2,1,0:T(8,128)} copy(f32[2,3,12,16,128]{4,3,2,1,0:T(8,128)} %bitcast.4) | data formatting | bytes 1179648
Async XLA Ops:
  0.0 0.7 copy-start
where the time goes:
time: 110 us; the launch traced here: 109 us
  Pallas kernels  106 us (96%)
  local copies, waits for them, and re-layouts  3.28 us (3%)
    pallas_call x1, Pallas kernels, local(): pl.pallas_call(functools.partial(kernel, size_x, size_y, names), out_shap...  106 us
    unnamed x4, local copies, waits for them, and re-layouts  3.28 us

commit v1 on v0

--- a/solution.py
+++ b/solution.py
@@ -20,7 +20,11 @@
 EX, EY = 3, 4
 DEGREES = (4, 2, 1)
 ROWS = (224, 64, 32)
-KPAD = (256, 128, 128)
+HALO = 2
+WHOLE = (224, 256, 96)
+MID = (224, 144, 64)
+KPAD = (256, 256, 128)
+FINE = (256, 128)
 LANES = (256, 128, 128)
 STEPS = (3, 3, 4)
 
@@ -69,6 +73,42 @@
     rows += [(px, y) for y in range(py + 1)]
     rows += [(x, py) for x in range(px)]
     return rows
+
+
+def halo_rows(degree, level):
+    nodes = dict(enumerate(node_rows(degree)))
+    places = {node: row for row, node in nodes.items()}
+    at = ROWS[level]
+    for ring in range(1, HALO + 1):
+        if ring == 2:
+            assert at <= MID[level]
+            at = max(at, 0)
+        w = ring * degree
+        for x in range(-w, EX * degree + w + 1):
+            for y in range(-w, EY * degree + w + 1):
+                if (x, y) not in places:
+                    places[x, y] = at
+                    at += 1
+    assert at <= WHOLE[level]
+    return places
+
+
+def segments(degree):
+    px, py, w = EX * degree, EY * degree, HALO * degree
+    spans = {-1: lambda n: range(0, w + 1), 0: lambda n: range(0, n + 1), 1: lambda n: range(n - w, n + 1)}
+    return [[(x, y) for x in spans[dx](px) for y in spans[dy](py)] for dx, dy in DIRS]
+
+
+def segment_starts(level):
+    starts, at = [], ROWS[level]
+    for nodes in segments(DEGREES[level]):
+        starts.append((at, rounded8(len(nodes))))
+        at += rounded8(len(nodes))
+    return starts, at
+
+
+def gathered(level):
+    return -(-segment_starts(level)[1] // 128) * 128
 
 
 def split(values, terms):
@@ -135,27 +175,65 @@
             hi, lo = split(wide, 2)
             stacks.append(np.concatenate([hi, hi, lo], 0))
         out["z", level] = np.stack(stacks)
+        places = {(x, y): r for r, (x, y) in enumerate(rows)}
+        if level:
+            places = halo_rows(degree, level)
+            w = HALO * degree
+            hx = np.zeros((MID[level], 16), np.float32)
+            hy = np.zeros((MID[level], 32), np.float32)
+            for (x, y), r in places.items():
+                if r < MID[level]:
+                    hx[r, x + w] = 1.0
+                    hy[r, y + w] = 1.0
+            out["hrx", level] = np.concatenate([hx] * 3, 1).astype(ml_dtypes.bfloat16)
+            out["hry", level] = np.concatenate([hy] * 3, 1).astype(ml_dtypes.bfloat16)
+            htx = np.zeros((4, 48, kpad), ml_dtypes.bfloat16)
+            hty = np.zeros((4, 96, kpad), ml_dtypes.bfloat16)
+            for op in range(4):
+                ex = assembled(mats[op], EX + 2 * HALO, False)
+                ey = assembled(mats[op], EY + 2 * HALO, False)
+                wide_x = np.zeros((16, kpad))
+                wide_y = np.zeros((32, kpad))
+                for (x, y), r in places.items():
+                    wide_x[: ex.shape[0], r] = ex[:, x + w]
+                    wide_y[: ey.shape[0], r] = ey[:, y + w]
+                htx[op] = np.concatenate(split(wide_x, 3), 0)
+                hty[op] = np.concatenate(split(wide_y, 3), 0)
+            out["htx", level], out["hty", level] = htx, hty
+            starts, total = segment_starts(level)
+            pack = np.zeros((total - n, 128), np.float32)
+            unpack = np.zeros((WHOLE[level], gathered(level)), np.float32)
+            for r in range(len(rows)):
+                unpack[r, r] = 1.0
+            for (begin, _), nodes, (dx, dy) in zip(starts, segments(degree), DIRS):
+                for k, (x, y) in enumerate(nodes):
+                    pack[begin - n + k, rows.index((x, y))] = 1.0
+                    unpack[places[x - dx * EX * degree, y - dy * EY * degree], begin + k] = 1.0
+            out["pk", level] = pack.astype(ml_dtypes.bfloat16)
+            out["un", level] = unpack.astype(ml_dtypes.bfloat16)
         weights = MU_SHEAR + CROSS * np.eye(3)
 
-        def center(op, count):
-            full = assembled(mats[op], count, True)
-            diag = np.array([full[i % degree, i % degree] for i in range(count * degree)])
-            diag[::degree] = mats[op][0, 0] + mats[op][degree, degree]
-            return np.append(diag, diag[0])
-
-        cx = [center(op, EX) for op in (0, 1)]
-        cy = [center(op, EY) for op in (0, 1)]
-        cz = [center(op, elements_z)[:nz] for op in (0, 1)]
-        kd = np.ones((3, n, 128), np.float32)
-        for c in range(3):
-            for r, (x, y) in enumerate(rows):
-                row = (
-                    weights[c, 0] * cx[1][x] * cy[0][y] * cz[0]
-                    + weights[c, 1] * cx[0][x] * cy[1][y] * cz[0]
-                    + weights[c, 2] * cx[0][x] * cy[0][y] * cz[1]
-                )
-                kd[c, r, : copies * nz] = np.tile(row, copies)
-        out["kd", level] = kd
+        def center(op, i):
+            return mats[op][i % degree, i % degree] + (mats[op][degree, degree] if i % degree == 0 else 0.0)
+
+        pairs = ((0, 0), (0, 1), (1, 0), (1, 1), (0, 2), (2, 0))
+        columns = np.zeros((3, WHOLE[level], 16), ml_dtypes.bfloat16)
+        lines = np.zeros((16, 128), ml_dtypes.bfloat16)
+        along = np.zeros((2, 128))
+        for op in (0, 1):
+            along[op, : copies * nz] = np.tile([center(op, z) for z in range(nz)], copies)
+        parts = split(along, 3)
+        for k, (_, i) in enumerate(pairs):
+            lines[2 * k : 2 * k + 2] = parts[i]
+        for c in range(3):
+            pair = np.ones((WHOLE[level], 2))
+            for (x, y), r in places.items():
+                pair[r, 0] = weights[c, 0] * center(1, x) * center(0, y) + weights[c, 1] * center(0, x) * center(1, y)
+                pair[r, 1] = weights[c, 2] * center(0, x) * center(0, y)
+            parts = split(pair, 3)
+            for k, (i, _) in enumerate(pairs):
+                columns[c, :, 2 * k : 2 * k + 2] = parts[i]
+        out["kc", level], out["kr", level] = columns, lines
         if level == 2:
             continue
         half = DEGREES[level + 1]
@@ -164,13 +242,18 @@
         px_, py_ = interpolation(degree, EX, True), interpolation(degree, EY, True)
         pz_ = interpolation(degree, elements_z, False)
         pxy = np.zeros((n, 128), np.float32)
-        sample = np.zeros((ROWS[level + 1], kpad), np.float32)
+        sample = np.zeros((ROWS[level + 1], FINE[level]), np.float32)
         for c, (xc, yc) in enumerate(coarse_rows):
             for r, (x, y) in enumerate(rows):
                 pxy[r, c] = px_[x, xc] * py_[y, yc]
             sample[c, rows.index((2 * xc, 2 * yc))] = 1.0
-        rxy = np.zeros((ROWS[level + 1], kpad), np.float32)
-        rxy[:, :n] = pxy[:, : ROWS[level + 1]].T
+        coarse = ROWS[level + 1]
+        starts, total = segment_starts(level + 1)
+        rxy = np.zeros((total, FINE[level]), np.float32)
+        rxy[:coarse, :n] = pxy[:, :coarse].T
+        for (begin, _), nodes in zip(starts, segments(half)):
+            for k, node in enumerate(nodes):
+                rxy[begin + k] = rxy[coarse_rows.index(node)]
         pz = np.zeros((128, lanes), np.float32)
         for v in range(VECS):
             pz[v * nzc : (v + 1) * nzc, v * nz : (v + 1) * nz] = pz_.T
@@ -259,7 +342,7 @@
             load(const_hbm[name], const[name])
 
     for level in range(3):
-        for name in ("recv_x", "recv_y", "recv_c"):
+        for name in ("recv_x", "recv_y", "recv_c") + (("wide_recv", "wide_send") if level else ()):
             ref = scratch[name, level]
             ref[...] = jnp.zeros_like(ref)
     for name in ("first_x", "first_y", "first_c"):
@@ -283,8 +366,7 @@
         ref[...] = jnp.zeros_like(ref)
         ref = state("zlo", level)
         ref[...] = jnp.zeros_like(ref)
-    for name in ("tmp_hi", "tmp_mid", "tmp_lo"):
-        scratch[name][...] = jnp.zeros_like(scratch[name])
+    scratch["tmp"][...] = jnp.zeros_like(scratch["tmp"])
     b0[:, own0:, :] = jnp.zeros((3, ROWS[0] - own0, 256), F32)
     m0, s0 = state("m", 0), state("s", 0)
     m0[own0:, :] = jnp.zeros((ROWS[0] - own0, 128), F32)
@@ -335,6 +417,81 @@
         @pl.when(exists(dx, dy))
         def _():
             first_copy(k).start()
+
+    def spread_copy(level, slot, d):
+        dx, dy = DIRS[d]
+        begin, length = segment_starts(level)[0][d]
+        n = ROWS[level]
+        return pltpu.make_async_remote_copy(
+            src_ref=state("wide_send", level).at[slot, :, begin - n : begin - n + length],
+            dst_ref=state("wide_recv", level).at[slot, :, begin : begin + length],
+            send_sem=scratch["wide_send_sem"].at[level, slot, d],
+            recv_sem=scratch["wide_recv_sem"].at[level, slot, d],
+            device_id=(ix + dx, iy + dy),
+            device_id_type=MESH,
+        )
+
+    def spread_start(level, slot):
+        for d in (4, 5, 6, 7, 0, 1, 2, 3):
+
+            @pl.when(exists(*DIRS[d]))
+            def _():
+                spread_copy(level, slot, d).start()
+
+    def spread_wait(level, slot):
+        for d in range(8):
+            dx, dy = DIRS[d]
+
+            @pl.when(exists(-dx, -dy))
+            def _():
+                spread_copy(level, slot, d).wait_recv()
+
+            @pl.when(exists(dx, dy))
+            def _():
+                spread_copy(level, slot, d).wait_send()
+
+    def pieces(value, count):
+        out, rest = [], value
+        for _ in range(count):
+            part = rest.astype(BF)
+            out.append(part)
+            rest = rest - part.astype(F32)
+        return out
+
+    def spread_values(level, slot, c, value, count):
+        n = ROWS[level]
+        hold = scratch["tmp"]
+        total = None
+        for k, part in enumerate(pieces(value, count)):
+            hold[k, 0:n, :] = part
+            got = dot(const["pk", level][...], hold[k, 0:128, :])
+            total = got if total is None else total + got
+        state("wide_send", level)[slot, c] = total
+        state("wide_recv", level)[slot, c, 0:n, :] = value
+
+    def collect(level, slot, c, first_row, count):
+        total = None
+        for part in pieces(state("wide_recv", level)[slot, c], count):
+            got = dot(const["un", level][first_row:, :], part)
+            total = got if total is None else total + got
+        return total
+
+    for copy in loads[n_first:]:
+        copy.wait()
+    for k, name in enumerate(("s", "m")):
+        value = state(name, 0)[...]
+        for level in (0, 1):
+            total = None
+            hold = scratch["tmp"]
+            n = ROWS[level]
+            for part in pieces(value, 3):
+                hold[0, 0:n, :] = dot(part, const["sz", level][...]).astype(BF)
+                got = dot(const["sxy", level][...], hold[0, 0 : FINE[level], :])
+                total = got if total is None else total + got
+            value = total
+            spread_values(level + 1, 0, k, value, 3)
+    for level in (1, 2):
+        spread_start(level, 0)
 
     coef = scratch["coef"]
     for level in range(3):
@@ -351,27 +508,28 @@
             coef[level * 8 + 2 * i + 1] = 2.0 * rho_next / radius
             rho = rho_next
 
-    for copy in loads[n_first:]:
-        copy.wait()
-
-    for level in range(3):
+    def matrices(level, halo):
         kpad = KPAD[level]
-        xe, ye = state("xe", level), state("ye", level)
+        n = MID[level] if halo else ROWS[level]
+        xe, ye = scratch["xe"], scratch["ye"]
+        h = "h" if halo else ""
         for op in range(4):
-            xe[op] = dot(const["rx", level][...], const["tx", level][op])
-            ye[op] = dot(const["ry", level][...], const["ty", level][op])
-        ahi, alo = state("ahi", level), state("alo", level)
+            xe[op, 0:n, 0:kpad] = dot(const[h + "rx", level][...], const[h + "tx", level][op])
+            ye[op, 0:n, 0:kpad] = dot(const[h + "ry", level][...], const[h + "ty", level][op])
+        ahi, alo = state(h + "ahi", level), state(h + "alo", level)
         for c in range(3):
             for j in range(4):
                 value = None
                 for factor, xop, yop in BLOCKS[c][j]:
-                    term = xe[xop] * ye[yop]
+                    term = xe[xop, 0:n, 0:kpad] * ye[yop, 0:n, 0:kpad]
                     if factor != 1.0:
                         term = factor * term
                     value = term if value is None else value + term
                 hi, lo = halves(value)
                 ahi[c, :, j * kpad : (j + 1) * kpad] = hi
                 alo[c, :, j * kpad : (j + 1) * kpad] = lo
+
+    matrices(0, False)
 
     for k in range(3):
         dx, dy = first[k][2]
@@ -395,50 +553,50 @@
         ref[208:209, :] = gc_[3:4, lane]
         ref[209:221, :] = gy_[36:48, lane]
 
-    for level in range(2):
-        kpad = KPAD[level]
-        n = ROWS[level]
-        for name in ("s", "m"):
-            rest = state(name, level)[...]
-            total = None
-            for term in range(1 if name == "m" else 3):
-                part = rest.astype(BF)
-                rest = rest - part.astype(F32)
-                scratch["tmp_hi"][0:n, :] = dot(part, const["sz", level][...]).astype(BF)
-                got = dot(const["sxy", level][...], scratch["tmp_hi"][0:kpad, :])
-                total = got if total is None else total + got
-            state(name, level + 1)[...] = total
-
     def wide(value, level):
         return jnp.concatenate([value, value], 1) if LANES[level] == 256 else value
 
-    for level in range(3):
+    def diagonal(level):
         s, m = state("s", level)[...], state("m", level)[...]
         for c in range(3):
-            state("dinv", level)[c] = 1.0 / (s * s * const["kd", level][c] + (1.0 - m))
-
-    def apply_partial(level, source, target):
-        n, kpad, lanes = ROWS[level], KPAD[level], LANES[level]
+            kd = dot(const["kc", level][c], const["kr", level][...])
+            state("dinv", level)[c] = 1.0 / (s * s * kd + (1.0 - m))
+
+    def coarse_setup():
+        for level in (1, 2):
+            matrices(level, False)
+            matrices(level, True)
+        for level in (1, 2):
+            spread_wait(level, 0)
+            for k, name in enumerate(("s", "m")):
+                state(name, level)[...] = collect(level, 0, k, 0, 3)
+            diagonal(level)
+
+    diagonal(0)
+
+    def apply(level, source, target, rows_in, rows_out, halo):
+        n, kpad, lanes = rows_in, KPAD[level], LANES[level]
         zhi, zlo = state("zhi", level), state("zlo", level)
-        s = state("s", level)[...]
+        s = state("s", level)[0:n, :]
         for c in range(3):
             ops = (M_, K_, T_ if c == 2 else G_)
             for h in range(lanes // 128):
                 lane = slice(128 * h, 128 * h + 128)
-                hi, lo = halves(s * source[c, :, lane])
+                hi, lo = halves(s * source[c, 0:n, lane])
                 prod = dot(jnp.concatenate([hi, lo, hi], 1), const["z", level][1 if c == 2 else 0])
                 for k, op in enumerate(ops):
                     slot = SLOT_OF[c, op]
                     zh, zl = halves(prod[:, 128 * k : 128 * k + 128])
                     zhi[slot * kpad : slot * kpad + n, lane] = zh
                     zlo[slot * kpad : slot * kpad + n, lane] = zl
-        ahi, alo = state("ahi", level), state("alo", level)
+        name = "h" if halo else ""
+        ahi, alo = state(name + "ahi", level), state(name + "alo", level)
         for c in range(3):
             span = slice(FIRST_SLOT[c] * kpad, (FIRST_SLOT[c] + 4) * kpad)
-            value = dot(ahi[c], zhi[span, :]) + dot(ahi[c], zlo[span, :]) + dot(alo[c], zhi[span, :])
-            target[c] = value
-
-    def exchange(level, slot, t):
+            hi, lo = ahi[c, 0:rows_out, :], alo[c, 0:rows_out, :]
+            target[c, 0:rows_out, :] = dot(hi, zhi[span, :]) + dot(hi, zlo[span, :]) + dot(lo, zhi[span, :])
+
+    def exchange(level, slot, t, meanwhile=None):
         p = DEGREES[level]
         px, py = EX * p, EY * p
         nown = px * py
@@ -475,6 +633,8 @@
             def _():
                 copy(d).start()
 
+        if meanwhile is not None:
+            meanwhile()
         for d in range(8):
             dx, dy = DIRS[d]
 
@@ -499,22 +659,20 @@
             def _():
                 copy(d).wait_send()
 
-    def step(level, i, slot):
+    def update(level, i, n):
         r, d, x, t = (state(name, level) for name in ("r", "d", "x", "t"))
-        apply_partial(level, d, t)
-        exchange(level, slot, t)
-        s = wide(state("s", level)[...], level)
-        f = 1.0 - wide(state("m", level)[...], level)
+        s = wide(state("s", level)[0:n, :], level)
+        f = 1.0 - wide(state("m", level)[0:n, :], level)
         lanes = LANES[level]
         alpha = coef[level * 8 + 2 * i][:, :lanes]
         beta = coef[level * 8 + 2 * i + 1][:, :lanes]
         for c in range(3):
-            old = d[c]
-            res = r[c] - (s * t[c] + f * old)
-            r[c] = res
-            new = alpha * old + beta * (wide(state("dinv", level)[c], level) * res)
-            d[c] = new
-            x[c] = x[c] + new
+            old = d[c, 0:n, :]
+            res = r[c, 0:n, :] - (s * t[c, 0:n, :] + f * old)
+            r[c, 0:n, :] = res
+            new = alpha * old + beta * (wide(state("dinv", level)[c, 0:n, :], level) * res)
+            d[c, 0:n, :] = new
+            x[c, 0:n, :] = x[c, 0:n, :] + new
 
     def start(level):
         b, r, d, x = (state(name, level) for name in ("b", "r", "d", "x"))
@@ -534,68 +692,111 @@
     def restrict(level, slot):
         n, n_next = ROWS[level], ROWS[level + 1]
         x, t, b = state("x", level), state("t", level), state("b", level)
-        apply_partial(level, x, t)
         p = DEGREES[level]
         nown = EX * p * EY * p
-        s = wide(state("s", level)[...], level)
-        m = wide(state("m", level)[...], level)
+        s = wide(state("s", level)[0:n, :], level)
+        m = wide(state("m", level)[0:n, :], level)
         rows = lax.broadcasted_iota(jnp.int32, (n, LANES[level]), 0)
         m = jnp.where(rows < nown, m, 0.0)
-        t_next = state("t", level + 1)
-        hi_ref, lo_ref = scratch["tmp_hi"], scratch["tmp_lo"]
-        for c in range(3):
-            y = m * b[c] - s * t[c]
-            hi, lo = halves(y)
-            yz = dot(jnp.concatenate([hi, lo], 1), const["rz", level][...])
-            hi, lo = halves(yz)
-            hi_ref[0:n, :] = hi
-            lo_ref[0:n, :] = lo
+        hold = scratch["tmp"]
+        for c in range(3):
+            hi, lo = halves(m * b[c, 0:n, :] - s * t[c, 0:n, :])
+            hi, lo = halves(dot(jnp.concatenate([hi, lo], 1), const["rz", level][...]))
+            hold[0, 0:n, :] = hi
+            hold[1, 0:n, :] = lo
             mat = const["rxy", level][...]
-            t_next[c] = dot(mat, hi_ref[0 : KPAD[level], :]) + dot(mat, lo_ref[0 : KPAD[level], :])
-        exchange(level + 1, slot, t_next)
+            value = dot(mat, hold[0, 0 : FINE[level], :]) + dot(mat, hold[1, 0 : FINE[level], :])
+            state("wide_recv", level + 1)[slot, c, 0:n_next, :] = value[0:n_next]
+            state("wide_send", level + 1)[slot, c] = value[n_next:]
+        spread_start(level + 1, slot)
+        spread_wait(level + 1, slot)
         m_next = state("m", level + 1)[...]
         for c in range(3):
-            state("b", level + 1)[c] = m_next * t_next[c]
+            state("b", level + 1)[c] = m_next * collect(level + 1, slot, c, 0, 2)
 
     def prolong(level):
-        n_next, lanes = ROWS[level + 1], LANES[level]
+        n, n_next, lanes = ROWS[level], ROWS[level + 1], LANES[level]
         e, x = state("x", level + 1), state("x", level)
-        m = wide(state("m", level)[...], level)
+        m = wide(state("m", level)[0:n, :], level)
         hi_ref, lo_ref = scratch["wide_hi"], scratch["wide_lo"]
         for c in range(3):
-            hi, lo = halves(e[c])
+            hi, lo = halves(e[c, 0:n_next, :])
             ez = dot(jnp.concatenate([hi, lo], 1), const["pz", level][...])
             hi, lo = halves(ez)
             hi_ref[0:n_next, 0:lanes] = hi
             lo_ref[0:n_next, 0:lanes] = lo
             mat = const["pxy", level][...]
             fine = dot(mat, hi_ref[:, 0:lanes]) + dot(mat, lo_ref[:, 0:lanes])
-            x[c] = x[c] + m * fine
+            x[c, 0:n, :] = x[c, 0:n, :] + m * fine
 
     for name in ("wide_hi", "wide_lo"):
         scratch[name][...] = jnp.zeros_like(scratch[name])
 
-    def steps(level, begin, end, first_exchange):
-        def body(i, carry):
-            step(level, i, lax.rem(first_exchange + i - begin, 2))
-            return carry
-
-        lax.fori_loop(begin, end, body, 0)
+    def near(level, source, i_first):
+        d, t = state("d", level), state("t", level)
+        apply(level, source, t, WHOLE[level], MID[level], True)
+        update(level, i_first, MID[level])
+        apply(level, d, t, MID[level], ROWS[level], True)
+        update(level, i_first + 1, ROWS[level])
+
+    def last(level, i):
+        n = ROWS[level]
+        apply(level, state("d", level), state("t", level), n, n, False)
+        exchange(level, 0, state("t", level))
+        update(level, i, n)
+
+    def coarse():
+        n = ROWS[1]
+        start(1)
+        near(1, state("d", 1), 1)
+        apply(1, state("x", 1), state("t", 1), n, n, False)
+        restrict(1, 1)
+        start(2)
+        near(2, state("d", 2), 1)
+        last(2, 3)
+        prolong(1)
+        x, nown = state("x", 1), EX * 2 * EY * 2
+        rows = lax.broadcasted_iota(jnp.int32, (n, 128), 0)
+        for c in range(3):
+            spread_values(1, 0, c, jnp.where(rows < nown, x[c, 0:n, :], 0.0), 2)
+        spread_start(1, 0)
+        spread_wait(1, 0)
+        for c in range(3):
+            x[c, n:, :] = collect(1, 0, c, n, 2)
+        restart(1)
+        near(1, state("d", 1), 0)
+        last(1, 2)
 
     start(0)
-    steps(0, 1, 3, 0)
-    restrict(0, 0)
-    start(1)
-    steps(1, 1, 3, 1)
-    restrict(1, 0)
-    start(2)
-    steps(2, 1, 4, 1)
-    prolong(1)
-    restart(1)
-    steps(1, 0, 3, 3)
-    prolong(0)
-    restart(0)
-    steps(0, 0, 3, 2)
+
+    def visit(i, carry):
+        n = ROWS[0]
+        d, t, x = state("d", 0), state("t", 0), state("x", 0)
+        apply(0, d, t, n, n, False)
+
+        @pl.when(i != 2)
+        def _():
+            def meanwhile():
+                pl.when(i == 0)(coarse_setup)
+
+            later = jnp.where(i > 2, 1, 0)
+            exchange(0, lax.rem(i - later, 2), t, meanwhile)
+            update(0, i + 1 - 4 * later, n)
+
+            @pl.when(i == 1)
+            def _():
+                d[...] = x[...]
+
+        @pl.when(i == 2)
+        def _():
+            restrict(0, 1)
+            coarse()
+            prolong(0)
+            restart(0)
+
+        return carry
+
+    lax.fori_loop(0, 6, visit, 0)
 
     x0 = state("x", 0)
     stores = []
@@ -618,16 +819,19 @@
             shape = shape[1:]
         items.append((("const", name), pltpu.VMEM(shape, dtype)))
     for level in range(3):
-        n, kpad, lanes = ROWS[level], KPAD[level], LANES[level]
+        n, kpad, lanes, whole = ROWS[level], KPAD[level], LANES[level], WHOLE[level]
         for name in ("b", "r", "d", "x", "t"):
-            items.append(((name, level), pltpu.VMEM((3, n, lanes), F32)))
-        items.append((("dinv", level), pltpu.VMEM((3, n, 128), F32)))
+            items.append(((name, level), pltpu.VMEM((3, whole, lanes), F32)))
+        items.append((("dinv", level), pltpu.VMEM((3, whole, 128), F32)))
         for name in ("s", "m"):
-            items.append(((name, level), pltpu.VMEM((n, 128), F32)))
-        for name in ("xe", "ye"):
-            items.append(((name, level), pltpu.VMEM((4, n, kpad), F32)))
+            items.append(((name, level), pltpu.VMEM((whole, 128), F32)))
         for name in ("ahi", "alo"):
             items.append(((name, level), pltpu.VMEM((3, n, 4 * kpad), BF)))
+            if level:
+                items.append((("h" + name, level), pltpu.VMEM((3, MID[level], 4 * kpad), BF)))
+        if level:
+            items.append((("wide_send", level), pltpu.VMEM((2, 3, segment_starts(level)[1] - n, 128), F32)))
+            items.append((("wide_recv", level), pltpu.VMEM((2, 3, gathered(level), 128), F32)))
         for name in ("zhi", "zlo"):
             items.append(((name, level), pltpu.VMEM((9 * kpad, lanes), BF)))
         nx, ny = rounded8(3 * (EY * DEGREES[level] + 1)), rounded8(3 * (EX * DEGREES[level] + 1))
@@ -639,8 +843,9 @@
         items.append((name + "_x", pltpu.VMEM((64, 256), F32)))
         items.append((name + "_y", pltpu.VMEM((48, 256), F32)))
         items.append((name + "_c", pltpu.VMEM((8, 256), F32)))
-    for name in ("tmp_hi", "tmp_mid", "tmp_lo"):
-        items.append((name, pltpu.VMEM((256, 128), BF)))
+    items.append(("tmp", pltpu.VMEM((3, 256, 128), BF)))
+    for name in ("xe", "ye"):
+        items.append((name, pltpu.VMEM((4, 224, 256), F32)))
     for name in ("wide_hi", "wide_lo"):
         items.append((name, pltpu.VMEM((128, 256), BF)))
     items.append(("w", pltpu.VMEM((EX * 4 * EY * 4, 128), F32)))
@@ -649,6 +854,8 @@
     items.append(("load", pltpu.SemaphoreType.DMA((8 + len(names),))))
     items.append(("send", pltpu.SemaphoreType.DMA((3, 2, 8))))
     items.append(("recv", pltpu.SemaphoreType.DMA((3, 2, 8))))
+    items.append(("wide_send_sem", pltpu.SemaphoreType.DMA((3, 2, 8))))
+    items.append(("wide_recv_sem", pltpu.SemaphoreType.DMA((3, 2, 8))))
     items.append(("first_send", pltpu.SemaphoreType.DMA((3,))))
     items.append(("first_recv", pltpu.SemaphoreType.DMA((3,))))
     return items

time: 110 us -> 96.8 us (0.88)
  Pallas kernels: 106 us -> 93.4 us
    pallas_call x1, Pallas kernels: 106 us -> 93.4 us  [local(): pl.pallas_call(functools.partial(kernel, size_x, size_y, names), out_shap...]
where the time goes in v1:
time: 96.8 us; the launch traced here: 96.7 us
  Pallas kernels  93.4 us (96%)
  local copies, waits for them, and re-layouts  3.28 us (3%)
    pallas_call x1, Pallas kernels, local(): pl.pallas_call(functools.partial(kernel, size_x, size_y, names), out_shap...  93.4 us
    unnamed x4, local copies, waits for them, and re-layouts  3.28 us

profile of v1, /device:TPU:25, one launch (start us, length us, event | category | flops | bytes accessed | tf_op | source)
XLA Modules:
  0.0 96.7 jit_solution(10497608350932501270)
XLA Ops:
  0.0 0.0 copy-start
  0.0 0.7 copy-done
  0.7 0.7 copy.50.refs_3_
  1.3 93.4 %shard_map.451 = f32[2,3,192,128]{3,2,1,0:T(8,128)} custom-call(f32[2,3,192,128]{3,2,1,0:T(8,128)} %bitcast.5, f32[192,128]{1,0:T(8,128)} %bitcast.6, s32[192,128]{1,0:T(8,128)} %bitcast.7, f32[3,2]{1,0:T(4,128)} %copy.50.refs_3_, bf16[224,48]{1,0:T(8,128)(2,1)} %constant.90.clone.refs_4_, bf16[224,96]{1,0:T(8,128)(2,1)} %constant.91.clone.refs_5_, ...), custom_call_target="tpu_custom_call" | custom-call | tf_op jit(solution)/shard_map/pallas_call | solution.py:878
  94.7 1.9 %copy.52 = f32[2,3,12,16,128]{4,3,2,1,0:T(8,128)} copy(f32[2,3,12,16,128]{4,3,2,1,0:T(8,128)} %bitcast.4) | data formatting | bytes 1179648
Async XLA Ops:
  0.0 0.7 copy-start

commit v2 on v1

--- a/solution.py
+++ b/solution.py
@@ -141,25 +141,25 @@
         mats = element_matrices(degree)
         nz = elements_z * degree
         pick_x = np.zeros((n, 16), np.float32)
-        pick_y = np.zeros((n, 32), np.float32)
+        pick_y = np.zeros((n, 24), np.float32)
         for r, (x, y) in enumerate(rows):
             pick_x[r, x] = 1.0
             pick_y[r, y] = 1.0
-        out["rx", level] = np.concatenate([pick_x] * 3, 1).astype(ml_dtypes.bfloat16)
-        out["ry", level] = np.concatenate([pick_y] * 3, 1).astype(ml_dtypes.bfloat16)
-        tx = np.zeros((2, 4, 48, kpad), ml_dtypes.bfloat16)
-        ty = np.zeros((2, 4, 96, kpad), ml_dtypes.bfloat16)
+        out["rx", level] = np.concatenate([pick_x] * 2, 1).astype(ml_dtypes.bfloat16)
+        out["ry", level] = np.concatenate([pick_y] * 2, 1).astype(ml_dtypes.bfloat16)
+        tx = np.zeros((2, 4, 32, kpad), ml_dtypes.bfloat16)
+        ty = np.zeros((2, 4, 48, kpad), ml_dtypes.bfloat16)
         for first in range(2):
             for op in range(4):
                 ex = assembled(mats[op], EX, first)
                 ey = assembled(mats[op], EY, first)
                 wide_x = np.zeros((16, kpad))
-                wide_y = np.zeros((32, kpad))
+                wide_y = np.zeros((24, kpad))
                 for c, (x, y) in enumerate(rows):
                     wide_x[: ex.shape[0], c] = ex[:, x]
                     wide_y[: ey.shape[0], c] = ey[:, y]
-                tx[first, op] = np.concatenate(split(wide_x, 3), 0)
-                ty[first, op] = np.concatenate(split(wide_y, 3), 0)
+                tx[first, op] = np.concatenate(split(wide_x, 2), 0)
+                ty[first, op] = np.concatenate(split(wide_y, 2), 0)
         out["tx", level], out["ty", level] = tx, ty
         copies = 1 if nz >= 128 else VECS
         zmats = []
@@ -169,36 +169,32 @@
             for v in range(copies):
                 block[v * nz : (v + 1) * nz, v * nz : (v + 1) * nz] = ez
             zmats.append(block)
-        stacks = []
-        for third in (2, 3):
-            wide = np.concatenate([zmats[0], zmats[1], zmats[third]], 1)
-            hi, lo = split(wide, 2)
-            stacks.append(np.concatenate([hi, hi, lo], 0))
-        out["z", level] = np.stack(stacks)
+        wide = np.concatenate([zmats[i] for i in (2, 0, 1, 3)], 1)
+        out["z", level] = np.concatenate(split(wide, 2), 0)
         places = {(x, y): r for r, (x, y) in enumerate(rows)}
         if level:
             places = halo_rows(degree, level)
             w = HALO * degree
             hx = np.zeros((MID[level], 16), np.float32)
-            hy = np.zeros((MID[level], 32), np.float32)
+            hy = np.zeros((MID[level], 24), np.float32)
             for (x, y), r in places.items():
                 if r < MID[level]:
                     hx[r, x + w] = 1.0
                     hy[r, y + w] = 1.0
-            out["hrx", level] = np.concatenate([hx] * 3, 1).astype(ml_dtypes.bfloat16)
-            out["hry", level] = np.concatenate([hy] * 3, 1).astype(ml_dtypes.bfloat16)
-            htx = np.zeros((4, 48, kpad), ml_dtypes.bfloat16)
-            hty = np.zeros((4, 96, kpad), ml_dtypes.bfloat16)
+            out["hrx", level] = np.concatenate([hx] * 2, 1).astype(ml_dtypes.bfloat16)
+            out["hry", level] = np.concatenate([hy] * 2, 1).astype(ml_dtypes.bfloat16)
+            htx = np.zeros((4, 32, kpad), ml_dtypes.bfloat16)
+            hty = np.zeros((4, 48, kpad), ml_dtypes.bfloat16)
             for op in range(4):
                 ex = assembled(mats[op], EX + 2 * HALO, False)
                 ey = assembled(mats[op], EY + 2 * HALO, False)
                 wide_x = np.zeros((16, kpad))
-                wide_y = np.zeros((32, kpad))
+                wide_y = np.zeros((24, kpad))
                 for (x, y), r in places.items():
                     wide_x[: ex.shape[0], r] = ex[:, x + w]
                     wide_y[: ey.shape[0], r] = ey[:, y + w]
-                htx[op] = np.concatenate(split(wide_x, 3), 0)
-                hty[op] = np.concatenate(split(wide_y, 3), 0)
+                htx[op] = np.concatenate(split(wide_x, 2), 0)
+                hty[op] = np.concatenate(split(wide_y, 2), 0)
             out["htx", level], out["hty", level] = htx, hty
             starts, total = segment_starts(level)
             pack = np.zeros((total - n, 128), np.float32)
@@ -264,8 +260,8 @@
         for name, value in (
             ("pxy", pxy),
             ("rxy", rxy),
-            ("pz", np.concatenate([pz, pz], 0)),
-            ("rz", np.concatenate([pz.T, pz.T], 0)),
+            ("pz", pz),
+            ("rz", pz.T),
             ("sxy", sample),
             ("sz", sample_z),
         ):
@@ -330,6 +326,7 @@
             load(modes.at[v, c], b0.at[c, 0:own0, v * 128 : (v + 1) * 128])
     load(moduli, scratch["w"])
     load(pinned, scratch["pin"])
+    load(spectrum, scratch["spec"])
     n_first = len(loads)
     edge_x = jnp.where(ix == 0, 1, 0)
     edge_y = jnp.where(iy == 0, 1, 0)
@@ -338,6 +335,13 @@
             load(const_hbm[name].at[edge_x], const[name])
         elif name[0] == "ty":
             load(const_hbm[name].at[edge_y], const[name])
+        elif name[0] == "z":
+            for begin, row in ((0, 0), (128, 0), (256, 128)):
+                load(const_hbm[name].at[row : row + 128], const[name].at[begin : begin + 128])
+        elif name[0] in ("pz", "rz"):
+            half = const_hbm[name].shape[0]
+            load(const_hbm[name], const[name].at[0:half])
+            load(const_hbm[name], const[name].at[half : 2 * half])
         else:
             load(const_hbm[name], const[name])
 
@@ -362,10 +366,11 @@
         for name in ("send_x", "send_y", "send_c"):
             ref = state(name, level)
             ref[...] = jnp.zeros_like(ref)
-        ref = state("zhi", level)
-        ref[...] = jnp.zeros_like(ref)
-        ref = state("zlo", level)
-        ref[...] = jnp.zeros_like(ref)
+        pad = KPAD[level] - WHOLE[level]
+        for slot in range(9 if pad else 0):
+            for name in ("zhi", "zlo"):
+                end = (slot + 1) * KPAD[level]
+                state(name, level)[end - pad : end, :] = jnp.zeros((pad, LANES[level]), BF)
     scratch["tmp"][...] = jnp.zeros_like(scratch["tmp"])
     b0[:, own0:, :] = jnp.zeros((3, ROWS[0] - own0, 256), F32)
     m0, s0 = state("m", 0), state("s", 0)
@@ -476,27 +481,27 @@
             total = got if total is None else total + got
         return total
 
-    for copy in loads[n_first:]:
-        copy.wait()
-    for k, name in enumerate(("s", "m")):
-        value = state(name, 0)[...]
-        for level in (0, 1):
-            total = None
-            hold = scratch["tmp"]
-            n = ROWS[level]
-            for part in pieces(value, 3):
-                hold[0, 0:n, :] = dot(part, const["sz", level][...]).astype(BF)
-                got = dot(const["sxy", level][...], hold[0, 0 : FINE[level], :])
-                total = got if total is None else total + got
-            value = total
-            spread_values(level + 1, 0, k, value, 3)
-    for level in (1, 2):
-        spread_start(level, 0)
+    def coarse_samples():
+        for k, name in enumerate(("s", "m")):
+            hold, value = scratch["tmp"], state(name, 0)[...]
+            rows = lax.broadcasted_iota(jnp.int32, value.shape, 0)
+            value = jnp.where(rows < own0, value, 0.0)
+            for level in (0, 1):
+                total = None
+                n = ROWS[level]
+                for part in pieces(value, 3):
+                    hold[0, 0:n, :] = dot(part, const["sz", level][...]).astype(BF)
+                    got = dot(const["sxy", level][...], hold[0, 0 : FINE[level], :])
+                    total = got if total is None else total + got
+                value = total
+                spread_values(level + 1, 0, k, value, 3)
+        for level in (1, 2):
+            spread_start(level, 0)
 
     coef = scratch["coef"]
     for level in range(3):
-        low = jnp.full((1, 256), spectrum[level, 0], F32)
-        top = jnp.full((1, 256), spectrum[level, 1], F32)
+        low = jnp.full((1, 256), scratch["spec"][0, level], F32)
+        top = jnp.full((1, 256), scratch["spec"][1, level], F32)
         center, radius = 0.5 * (top + low), 0.5 * (top - low)
         sigma = center / radius
         rho = 1.0 / sigma
@@ -529,6 +534,8 @@
                 ahi[c, :, j * kpad : (j + 1) * kpad] = hi
                 alo[c, :, j * kpad : (j + 1) * kpad] = lo
 
+    for copy in loads[n_first:]:
+        copy.wait()
     matrices(0, False)
 
     for k in range(3):
@@ -562,10 +569,13 @@
             kd = dot(const["kc", level][c], const["kr", level][...])
             state("dinv", level)[c] = 1.0 / (s * s * kd + (1.0 - m))
 
-    def coarse_setup():
+    def coarse_matrices():
+        coarse_samples()
         for level in (1, 2):
             matrices(level, False)
             matrices(level, True)
+
+    def coarse_coefficients():
         for level in (1, 2):
             spread_wait(level, 0)
             for k, name in enumerate(("s", "m")):
@@ -579,11 +589,11 @@
         zhi, zlo = state("zhi", level), state("zlo", level)
         s = state("s", level)[0:n, :]
         for c in range(3):
-            ops = (M_, K_, T_ if c == 2 else G_)
+            ops = (M_, K_, T_) if c == 2 else (G_, M_, K_)
             for h in range(lanes // 128):
                 lane = slice(128 * h, 128 * h + 128)
                 hi, lo = halves(s * source[c, 0:n, lane])
-                prod = dot(jnp.concatenate([hi, lo, hi], 1), const["z", level][1 if c == 2 else 0])
+                prod = dot(jnp.concatenate([hi, lo, hi], 1), const["z", level][:, 128:] if c == 2 else const["z", level][:, 0:384])
                 for k, op in enumerate(ops):
                     slot = SLOT_OF[c, op]
                     zh, zl = halves(prod[:, 128 * k : 128 * k + 128])
@@ -777,7 +787,8 @@
         @pl.when(i != 2)
         def _():
             def meanwhile():
-                pl.when(i == 0)(coarse_setup)
+                pl.when(i == 0)(coarse_matrices)
+                pl.when(i == 1)(coarse_coefficients)
 
             later = jnp.where(i > 2, 1, 0)
             exchange(0, lax.rem(i - later, 2), t, meanwhile)
@@ -817,6 +828,10 @@
         shape, dtype = shapes[name]
         if name[0] in ("tx", "ty"):
             shape = shape[1:]
+        if name[0] == "z":
+            shape = (384, 512)
+        if name[0] in ("pz", "rz"):
+            shape = (2 * shape[0], shape[1])
         items.append((("const", name), pltpu.VMEM(shape, dtype)))
     for level in range(3):
         n, kpad, lanes, whole = ROWS[level], KPAD[level], LANES[level], WHOLE[level]
@@ -850,8 +865,9 @@
         items.append((name, pltpu.VMEM((128, 256), BF)))
     items.append(("w", pltpu.VMEM((EX * 4 * EY * 4, 128), F32)))
     items.append(("pin", pltpu.VMEM((EX * 4 * EY * 4, 128), jnp.int32)))
+    items.append(("spec", pltpu.SMEM((2, 3), F32)))
     items.append(("coef", pltpu.VMEM((24, 1, 256), F32)))
-    items.append(("load", pltpu.SemaphoreType.DMA((8 + len(names),))))
+    items.append(("load", pltpu.SemaphoreType.DMA((24 + len(names),))))
     items.append(("send", pltpu.SemaphoreType.DMA((3, 2, 8))))
     items.append(("recv", pltpu.SemaphoreType.DMA((3, 2, 8))))
     items.append(("wide_send_sem", pltpu.SemaphoreType.DMA((3, 2, 8))))
@@ -878,7 +894,7 @@
         out = pl.pallas_call(
             functools.partial(kernel, size_x, size_y, names),
             out_shape=jax.ShapeDtypeStruct((VECS, 3, own, 128), F32),
-            in_specs=[any_spec] * 3 + [pl.BlockSpec(memory_space=pltpu.SMEM)] + [any_spec] * len(names),
+            in_specs=[any_spec] * (4 + len(names)),
             out_specs=any_spec,
             scratch_shapes=[item for _, item in scratch_list(names, shapes)],
             compiler_params=pltpu.CompilerParams(
@@ -888,7 +904,7 @@
             modes.reshape(VECS, 3, own, 128),
             moduli.reshape(own, 128),
             pinned.reshape(own, 128),
-            spectrum,
+            spectrum.T,
             *[jnp.asarray(tables[name]) for name in names],
         )
         return out.reshape(modes.shape)

time: 96.8 us -> 94.2 us (0.973)
  local copies, waits for them, and re-layouts: 3.28 us -> 1.94 us
  Pallas kernels: 93.4 us -> 92.2 us
    unnamed x4 -> x1, local copies, waits for them, and re-layouts: 3.28 us -> 1.94 us
    pallas_call x1, Pallas kernels: 93.4 us -> 92.2 us  [local(): pl.pallas_call(functools.partial(kernel, size_x, size_y, names), out_shap...]
where the time goes in v2:
time: 94.2 us; the launch traced here: 94.1 us
  Pallas kernels  92.2 us (98%)
  local copies, waits for them, and re-layouts  1.94 us (2%)
    pallas_call x1, Pallas kernels, local(): pl.pallas_call(functools.partial(kernel, size_x, size_y, names), out_shap...  92.2 us
    unnamed x1, local copies, waits for them, and re-layouts  1.94 us

profile of v2, /device:TPU:25, one launch (start us, length us, event | category | flops | bytes accessed | tf_op | source)
XLA Modules:
  0.0 94.1 jit_solution(8176268997995261900)
XLA Ops:
  0.0 92.2 %shard_map.451 = f32[2,3,192,128]{3,2,1,0:T(8,128)} custom-call(f32[2,3,192,128]{3,2,1,0:T(8,128)} %bitcast.6, f32[192,128]{1,0:T(8,128)} %bitcast.7, s32[192,128]{1,0:T(8,128)} %bitcast.8, f32[2,3]{1,0:T(2,128)} %bitcast.9, bf16[224,32]{1,0:T(8,128)(2,1)} %constant.90.clone.refs_4_, bf16[224,48]{1,0:T(8,128)(2,1)} %constant.91.clone.refs_5_, ...), custom_call_target="tpu_custom_call" | custom-call | tf_op jit(solution)/shard_map/pallas_call | solution.py:894
  92.2 1.9 %copy.51 = f32[2,3,12,16,128]{4,3,2,1,0:T(8,128)} copy(f32[2,3,12,16,128]{4,3,2,1,0:T(8,128)} %bitcast.5) | data formatting | bytes 1179648

commit v3 on v2

--- a/solution.py
+++ b/solution.py
@@ -20,9 +20,9 @@
 EX, EY = 3, 4
 DEGREES = (4, 2, 1)
 ROWS = (224, 64, 32)
-HALO = 2
-WHOLE = (224, 256, 96)
-MID = (224, 144, 64)
+HALO = (0, 2, 3)
+WHOLE = (224, 256, 128)
+RINGS = ((224,), (256, 144, 64), (128, 96, 64, 32))
 KPAD = (256, 256, 128)
 FINE = (256, 128)
 LANES = (256, 128, 128)
@@ -34,6 +34,8 @@
 }
 
 DIRS = ((-1, 0), (1, 0), (0, -1), (0, 1), (-1, -1), (1, 1), (1, -1), (-1, 1))
+FAR = ((-2, 0), (2, 0), (-2, -1), (2, 1), (2, -1), (-2, 1))
+SPREAD = ((), DIRS, DIRS + FAR)
 
 
 def element_matrices(degree):
@@ -79,29 +81,56 @@
     nodes = dict(enumerate(node_rows(degree)))
     places = {node: row for row, node in nodes.items()}
     at = ROWS[level]
-    for ring in range(1, HALO + 1):
-        if ring == 2:
-            assert at <= MID[level]
-            at = max(at, 0)
+    for ring in range(1, HALO[level] + 1):
         w = ring * degree
         for x in range(-w, EX * degree + w + 1):
             for y in range(-w, EY * degree + w + 1):
                 if (x, y) not in places:
                     places[x, y] = at
                     at += 1
-    assert at <= WHOLE[level]
+        assert at <= RINGS[level][-1 - ring]
     return places
 
 
-def segments(degree):
-    px, py, w = EX * degree, EY * degree, HALO * degree
-    spans = {-1: lambda n: range(0, w + 1), 0: lambda n: range(0, n + 1), 1: lambda n: range(n - w, n + 1)}
-    return [[(x, y) for x in spans[dx](px) for y in spans[dy](py)] for dx, dy in DIRS]
+def segments(level):
+    degree = DEGREES[level]
+    px, py, w = EX * degree, EY * degree, HALO[level] * degree
+
+    def span(n, step):
+        return [i for i in range(n + 1) if -w <= i - step * n <= n + w]
+
+    return [[(x, y) for x in span(px, dx) for y in span(py, dy)] for dx, dy in SPREAD[level]]
+
+
+def messages(degree):
+    px, py = EX * degree, EY * degree
+    long_, short = rounded8(py + 1), rounded8(px + 1)
+    down = [(px, 0)] + [(x, 0) for x in range(px)]
+    up = [(px, py)] + [(x, py) for x in range(px)]
+    return (
+        ([(0, y) for y in range(py + 1)], long_),
+        ([(px, y) for y in range(py + 1)], long_),
+        (down, short),
+        (up, short),
+    )
+
+
+def message_rows(level):
+    faces = messages(DEGREES[level])
+    spans, at = [], 0
+    for _, length in faces:
+        spans.append((at, at, length))
+        at += length
+    sent, last = at, faces[0][1] - 8
+    for begin in (0, spans[1][0] + last, spans[1][0], last):
+        spans.append((begin, at, 8))
+        at += 8
+    return spans, sent, at
 
 
 def segment_starts(level):
     starts, at = [], ROWS[level]
-    for nodes in segments(DEGREES[level]):
+    for nodes in segments(level):
         starts.append((at, rounded8(len(nodes))))
         at += rounded8(len(nodes))
     return starts, at
@@ -147,6 +176,16 @@
             pick_y[r, y] = 1.0
         out["rx", level] = np.concatenate([pick_x] * 2, 1).astype(ml_dtypes.bfloat16)
         out["ry", level] = np.concatenate([pick_y] * 2, 1).astype(ml_dtypes.bfloat16)
+        if level < 2:
+            spans, sent, _ = message_rows(level)
+            send_x = np.zeros((sent, 16), np.float32)
+            send_y = np.zeros((sent, 24), np.float32)
+            for (begin, _, _), (nodes, _) in zip(spans, messages(degree)):
+                for k, (x, y) in enumerate(nodes):
+                    send_x[begin + k, x] = 1.0
+                    send_y[begin + k, y] = 1.0
+            out["srx", level] = np.concatenate([send_x] * 2, 1).astype(ml_dtypes.bfloat16)
+            out["sry", level] = np.concatenate([send_y] * 2, 1).astype(ml_dtypes.bfloat16)
         tx = np.zeros((2, 4, 32, kpad), ml_dtypes.bfloat16)
         ty = np.zeros((2, 4, 48, kpad), ml_dtypes.bfloat16)
         for first in range(2):
@@ -161,6 +200,9 @@
                 tx[first, op] = np.concatenate(split(wide_x, 2), 0)
                 ty[first, op] = np.concatenate(split(wide_y, 2), 0)
         out["tx", level], out["ty", level] = tx, ty
+        if level == 2:
+            for name in ("rx", "ry", "tx", "ty"):
+                del out[name, level]
         copies = 1 if nz >= 128 else VECS
         zmats = []
         for op in range(4):
@@ -174,11 +216,12 @@
         places = {(x, y): r for r, (x, y) in enumerate(rows)}
         if level:
             places = halo_rows(degree, level)
-            w = HALO * degree
-            hx = np.zeros((MID[level], 16), np.float32)
-            hy = np.zeros((MID[level], 24), np.float32)
+            w = HALO[level] * degree
+            mid = RINGS[level][1]
+            hx = np.zeros((mid, 16), np.float32)
+            hy = np.zeros((mid, 24), np.float32)
             for (x, y), r in places.items():
-                if r < MID[level]:
+                if r < mid:
                     hx[r, x + w] = 1.0
                     hy[r, y + w] = 1.0
             out["hrx", level] = np.concatenate([hx] * 2, 1).astype(ml_dtypes.bfloat16)
@@ -186,8 +229,8 @@
             htx = np.zeros((4, 32, kpad), ml_dtypes.bfloat16)
             hty = np.zeros((4, 48, kpad), ml_dtypes.bfloat16)
             for op in range(4):
-                ex = assembled(mats[op], EX + 2 * HALO, False)
-                ey = assembled(mats[op], EY + 2 * HALO, False)
+                ex = assembled(mats[op], EX + 2 * HALO[level], False)
+                ey = assembled(mats[op], EY + 2 * HALO[level], False)
                 wide_x = np.zeros((16, kpad))
                 wide_y = np.zeros((24, kpad))
                 for (x, y), r in places.items():
@@ -201,7 +244,7 @@
             unpack = np.zeros((WHOLE[level], gathered(level)), np.float32)
             for r in range(len(rows)):
                 unpack[r, r] = 1.0
-            for (begin, _), nodes, (dx, dy) in zip(starts, segments(degree), DIRS):
+            for (begin, _), nodes, (dx, dy) in zip(starts, segments(level), SPREAD[level]):
                 for k, (x, y) in enumerate(nodes):
                     pack[begin - n + k, rows.index((x, y))] = 1.0
                     unpack[places[x - dx * EX * degree, y - dy * EY * degree], begin + k] = 1.0
@@ -247,7 +290,7 @@
         starts, total = segment_starts(level + 1)
         rxy = np.zeros((total, FINE[level]), np.float32)
         rxy[:coarse, :n] = pxy[:, :coarse].T
-        for (begin, _), nodes in zip(starts, segments(half)):
+        for (begin, _), nodes in zip(starts, segments(level + 1)):
             for k, node in enumerate(nodes):
                 rxy[begin + k] = rxy[coarse_rows.index(node)]
         pz = np.zeros((128, lanes), np.float32)
@@ -346,7 +389,7 @@
             load(const_hbm[name], const[name])
 
     for level in range(3):
-        for name in ("recv_x", "recv_y", "recv_c") + (("wide_recv", "wide_send") if level else ()):
+        for name in (("recv",) if level < 2 else ()) + (("wide_recv", "wide_send") if level else ()):
             ref = scratch[name, level]
             ref[...] = jnp.zeros_like(ref)
     for name in ("first_x", "first_y", "first_c"):
@@ -354,7 +397,7 @@
 
     barrier = pltpu.get_barrier_semaphore()
     count = jnp.int32(0)
-    for dx, dy in DIRS:
+    for dx, dy in DIRS + FAR:
         here = exists(dx, dy)
         count = count + jnp.where(here, 1, 0)
 
@@ -363,9 +406,6 @@
             pl.semaphore_signal(barrier, inc=1, device_id=(ix + dx, iy + dy), device_id_type=MESH)
 
     for level in range(3):
-        for name in ("send_x", "send_y", "send_c"):
-            ref = state(name, level)
-            ref[...] = jnp.zeros_like(ref)
         pad = KPAD[level] - WHOLE[level]
         for slot in range(9 if pad else 0):
             for name in ("zhi", "zlo"):
@@ -424,7 +464,7 @@
             first_copy(k).start()
 
     def spread_copy(level, slot, d):
-        dx, dy = DIRS[d]
+        dx, dy = SPREAD[level][d]
         begin, length = segment_starts(level)[0][d]
         n = ROWS[level]
         return pltpu.make_async_remote_copy(
@@ -437,15 +477,15 @@
         )
 
     def spread_start(level, slot):
-        for d in (4, 5, 6, 7, 0, 1, 2, 3):
-
-            @pl.when(exists(*DIRS[d]))
+        for d in reversed(range(len(SPREAD[level]))):
+
+            @pl.when(exists(*SPREAD[level][d]))
             def _():
                 spread_copy(level, slot, d).start()
 
     def spread_wait(level, slot):
-        for d in range(8):
-            dx, dy = DIRS[d]
+        for d in range(len(SPREAD[level])):
+            dx, dy = SPREAD[level][d]
 
             @pl.when(exists(-dx, -dy))
             def _():
@@ -513,14 +553,14 @@
             coef[level * 8 + 2 * i + 1] = 2.0 * rho_next / radius
             rho = rho_next
 
-    def matrices(level, halo):
+    def matrices(level, h):
         kpad = KPAD[level]
-        n = MID[level] if halo else ROWS[level]
+        n = const[h + "rx", level].shape[0]
         xe, ye = scratch["xe"], scratch["ye"]
-        h = "h" if halo else ""
+        table = "h" if h == "h" else ""
         for op in range(4):
-            xe[op, 0:n, 0:kpad] = dot(const[h + "rx", level][...], const[h + "tx", level][op])
-            ye[op, 0:n, 0:kpad] = dot(const[h + "ry", level][...], const[h + "ty", level][op])
+            xe[op, 0:n, 0:kpad] = dot(const[h + "rx", level][...], const[table + "tx", level][op])
+            ye[op, 0:n, 0:kpad] = dot(const[h + "ry", level][...], const[table + "ty", level][op])
         ahi, alo = state(h + "ahi", level), state(h + "alo", level)
         for c in range(3):
             for j in range(4):
@@ -536,7 +576,8 @@
 
     for copy in loads[n_first:]:
         copy.wait()
-    matrices(0, False)
+    matrices(0, "")
+    matrices(0, "s")
 
     for k in range(3):
         dx, dy = first[k][2]
@@ -571,9 +612,8 @@
 
     def coarse_matrices():
         coarse_samples()
-        for level in (1, 2):
-            matrices(level, False)
-            matrices(level, True)
+        for level, kind in ((1, "h"), (1, ""), (1, "s"), (2, "h")):
+            matrices(level, kind)
 
     def coarse_coefficients():
         for level in (1, 2):
@@ -584,8 +624,8 @@
 
     diagonal(0)
 
-    def apply(level, source, target, rows_in, rows_out, halo):
-        n, kpad, lanes = rows_in, KPAD[level], LANES[level]
+    def along_z(level, source, n):
+        kpad, lanes = KPAD[level], LANES[level]
         zhi, zlo = state("zhi", level), state("zlo", level)
         s = state("s", level)[0:n, :]
         for c in range(3):
@@ -593,81 +633,74 @@
             for h in range(lanes // 128):
                 lane = slice(128 * h, 128 * h + 128)
                 hi, lo = halves(s * source[c, 0:n, lane])
-                prod = dot(jnp.concatenate([hi, lo, hi], 1), const["z", level][:, 128:] if c == 2 else const["z", level][:, 0:384])
+                table = const["z", level][:, 128:] if c == 2 else const["z", level][:, 0:384]
+                prod = dot(jnp.concatenate([hi, lo, hi], 1), table)
                 for k, op in enumerate(ops):
                     slot = SLOT_OF[c, op]
                     zh, zl = halves(prod[:, 128 * k : 128 * k + 128])
                     zhi[slot * kpad : slot * kpad + n, lane] = zh
                     zlo[slot * kpad : slot * kpad + n, lane] = zl
-        name = "h" if halo else ""
-        ahi, alo = state(name + "ahi", level), state(name + "alo", level)
+
+    def across(level, kind, target, n):
+        kpad = KPAD[level]
+        zhi, zlo = state("zhi", level), state("zlo", level)
+        ahi, alo = state(kind + "ahi", level), state(kind + "alo", level)
         for c in range(3):
             span = slice(FIRST_SLOT[c] * kpad, (FIRST_SLOT[c] + 4) * kpad)
-            hi, lo = ahi[c, 0:rows_out, :], alo[c, 0:rows_out, :]
-            target[c, 0:rows_out, :] = dot(hi, zhi[span, :]) + dot(hi, zlo[span, :]) + dot(lo, zhi[span, :])
-
-    def exchange(level, slot, t, meanwhile=None):
+            hi, lo = ahi[c, 0:n, :], alo[c, 0:n, :]
+            target[c, 0:n, :] = dot(hi, zhi[span, :]) + dot(hi, zlo[span, :]) + dot(lo, zhi[span, :])
+
+    def face_copy(level, slot, d):
+        dx, dy = DIRS[d]
+        begin, there, length = message_rows(level)[0][d]
+        return pltpu.make_async_remote_copy(
+            src_ref=state("send", level).at[slot, :, begin : begin + length],
+            dst_ref=state("recv", level).at[slot, :, there : there + length],
+            send_sem=send_sems.at[level, slot, d],
+            recv_sem=recv_sems.at[level, slot, d],
+            device_id=(ix + dx, iy + dy),
+            device_id_type=MESH,
+        )
+
+    def send_faces(level, slot):
+        across(level, "s", state("send", level).at[slot], message_rows(level)[1])
+        for d in (4, 5, 6, 7, 0, 1, 2, 3):
+
+            @pl.when(exists(*DIRS[d]))
+            def _():
+                face_copy(level, slot, d).start()
+
+    def add_faces(level, slot, t):
         p = DEGREES[level]
         px, py = EX * p, EY * p
         nown = px * py
         nx, ny = py + 1, px + 1
-        sx, sy, sc = state("send_x", level), state("send_y", level), state("send_c", level)
-        rx, ry, rc = state("recv_x", level), state("recv_y", level), state("recv_c", level)
+        got = state("recv", level)
         corner = nown + py
-        for c in range(3):
-            sx[slot, 0, c * nx : c * nx + py, :] = t[c, 0:py, :]
-            sx[slot, 0, c * nx + py : c * nx + nx, :] = t[c, corner + 1 : corner + 2, :]
-            sx[slot, 1, c * nx : c * nx + nx, :] = t[c, nown : nown + nx, :]
-            sy[slot, 0, c * ny : c * ny + 1, :] = t[c, nown : nown + 1, :]
+        for d in range(8):
+            dx, dy = DIRS[d]
+
+            @pl.when(exists(-dx, -dy))
+            def _():
+                face_copy(level, slot, d).wait_recv()
+
+        at = [span[1] for span in message_rows(level)[0]]
+        for c in range(3):
+            t[c, nown : nown + nx, :] += got[slot, c, at[0] : at[0] + nx, :]
+            t[c, 0:py, :] += got[slot, c, at[1] : at[1] + py, :]
+            t[c, corner + 1 : corner + 2, :] += got[slot, c, at[1] + py : at[1] + nx, :]
+            t[c, corner : corner + ny, :] += got[slot, c, at[2] : at[2] + ny, :]
+            t[c, nown : nown + 1, :] += got[slot, c, at[3] : at[3] + 1, :]
             for x in range(px):
-                sy[slot, 0, c * ny + 1 + x : c * ny + 2 + x, :] = t[c, x * py : x * py + 1, :]
-            sy[slot, 1, c * ny : c * ny + ny, :] = t[c, corner : corner + ny, :]
-            for k, row in enumerate((0, corner, nown, corner + 1)):
-                sc[slot, k, c : c + 1, :] = t[c, row : row + 1, :]
-
-        def copy(d):
-            dx, dy = DIRS[d]
-            src, dst, k = ((sx, rx, d), (sy, ry, d - 2), (sc, rc, d - 4))[0 if d < 2 else 1 if d < 4 else 2]
-            return pltpu.make_async_remote_copy(
-                src_ref=src.at[slot, k],
-                dst_ref=dst.at[slot, k],
-                send_sem=send_sems.at[level, slot, d],
-                recv_sem=recv_sems.at[level, slot, d],
-                device_id=(ix + dx, iy + dy),
-                device_id_type=MESH,
-            )
-
-        for d in (2, 3, 4, 5, 6, 7, 0, 1):
+                t[c, x * py : x * py + 1, :] += got[slot, c, at[3] + 1 + x : at[3] + 2 + x, :]
+            for k, row in enumerate((corner, 0, corner + 1, nown)):
+                t[c, row : row + 1, :] += got[slot, c, at[4 + k] : at[4 + k] + 1, :]
+
+        for d in range(8):
 
             @pl.when(exists(*DIRS[d]))
             def _():
-                copy(d).start()
-
-        if meanwhile is not None:
-            meanwhile()
-        for d in range(8):
-            dx, dy = DIRS[d]
-
-            @pl.when(exists(-dx, -dy))
-            def _():
-                copy(d).wait_recv()
-
-        for c in range(3):
-            t[c, nown : nown + nx, :] += rx[slot, 0, c * nx : c * nx + nx, :]
-            t[c, 0:py, :] += rx[slot, 1, c * nx : c * nx + py, :]
-            t[c, corner + 1 : corner + 2, :] += rx[slot, 1, c * nx + py : c * nx + nx, :]
-            t[c, corner : corner + ny, :] += ry[slot, 0, c * ny : c * ny + ny, :]
-            t[c, nown : nown + 1, :] += ry[slot, 1, c * ny : c * ny + 1, :]
-            for x in range(px):
-                t[c, x * py : x * py + 1, :] += ry[slot, 1, c * ny + 1 + x : c * ny + 2 + x, :]
-            for k, row in enumerate((corner, 0, corner + 1, nown)):
-                t[c, row : row + 1, :] += rc[slot, k, c : c + 1, :]
-
-        for d in range(8):
-
-            @pl.when(exists(*DIRS[d]))
-            def _():
-                copy(d).wait_send()
+                face_copy(level, slot, d).wait_send()
 
     def update(level, i, n):
         r, d, x, t = (state(name, level) for name in ("r", "d", "x", "t"))
@@ -743,27 +776,29 @@
         scratch[name][...] = jnp.zeros_like(scratch[name])
 
     def near(level, source, i_first):
-        d, t = state("d", level), state("t", level)
-        apply(level, source, t, WHOLE[level], MID[level], True)
-        update(level, i_first, MID[level])
-        apply(level, d, t, MID[level], ROWS[level], True)
-        update(level, i_first + 1, ROWS[level])
+        t = state("t", level)
+        for k, (rows_in, rows_out) in enumerate(zip(RINGS[level], RINGS[level][1:])):
+            along_z(level, source, rows_in)
+            across(level, "h", t, rows_out)
+            update(level, i_first + k, rows_out)
 
     def last(level, i):
-        n = ROWS[level]
-        apply(level, state("d", level), state("t", level), n, n, False)
-        exchange(level, 0, state("t", level))
+        n, t = ROWS[level], state("t", level)
+        along_z(level, state("d", level), n)
+        send_faces(level, 0)
+        across(level, "", t, n)
+        add_faces(level, 0, t)
         update(level, i, n)
 
     def coarse():
         n = ROWS[1]
         start(1)
         near(1, state("d", 1), 1)
-        apply(1, state("x", 1), state("t", 1), n, n, False)
+        along_z(1, state("x", 1), n)
+        across(1, "", state("t", 1), n)
         restrict(1, 1)
         start(2)
         near(2, state("d", 2), 1)
-        last(2, 3)
         prolong(1)
         x, nown = state("x", 1), EX * 2 * EY * 2
         rows = lax.broadcasted_iota(jnp.int32, (n, 128), 0)
@@ -782,16 +817,21 @@
     def visit(i, carry):
         n = ROWS[0]
         d, t, x = state("d", 0), state("t", 0), state("x", 0)
-        apply(0, d, t, n, n, False)
+        later = jnp.where(i > 2, 1, 0)
+        slot = lax.rem(i - later, 2)
+        along_z(0, d, n)
 
         @pl.when(i != 2)
         def _():
-            def meanwhile():
-                pl.when(i == 0)(coarse_matrices)
-                pl.when(i == 1)(coarse_coefficients)
-
-            later = jnp.where(i > 2, 1, 0)
-            exchange(0, lax.rem(i - later, 2), t, meanwhile)
+            send_faces(0, slot)
+
+        across(0, "", t, n)
+
+        @pl.when(i != 2)
+        def _():
+            pl.when(i == 0)(coarse_matrices)
+            pl.when(i == 1)(coarse_coefficients)
+            add_faces(0, slot, t)
             update(0, i + 1 - 4 * later, n)
 
             @pl.when(i == 1)
@@ -840,20 +880,20 @@
         items.append((("dinv", level), pltpu.VMEM((3, whole, 128), F32)))
         for name in ("s", "m"):
             items.append(((name, level), pltpu.VMEM((whole, 128), F32)))
-        for name in ("ahi", "alo"):
-            items.append(((name, level), pltpu.VMEM((3, n, 4 * kpad), BF)))
-            if level:
-                items.append((("h" + name, level), pltpu.VMEM((3, MID[level], 4 * kpad), BF)))
+        sent, got = message_rows(level)[1:]
+        for kind, count in (("", n), ("s", sent), ("h", RINGS[level][1] if level else 0)):
+            if (level == 2 and kind != "h") or not count:
+                continue
+            for name in ("ahi", "alo"):
+                items.append(((kind + name, level), pltpu.VMEM((3, count, 4 * kpad), BF)))
+        if level < 2:
+            items.append((("send", level), pltpu.VMEM((2, 3, sent, lanes), F32)))
+            items.append((("recv", level), pltpu.VMEM((2, 3, got, lanes), F32)))
         if level:
             items.append((("wide_send", level), pltpu.VMEM((2, 3, segment_starts(level)[1] - n, 128), F32)))
             items.append((("wide_recv", level), pltpu.VMEM((2, 3, gathered(level), 128), F32)))
         for name in ("zhi", "zlo"):
             items.append(((name, level), pltpu.VMEM((9 * kpad, lanes), BF)))
-        nx, ny = rounded8(3 * (EY * DEGREES[level] + 1)), rounded8(3 * (EX * DEGREES[level] + 1))
-        for name in ("send", "recv"):
-            items.append(((name + "_x", level), pltpu.VMEM((2, 2, nx, lanes), F32)))
-            items.append(((name + "_y", level), pltpu.VMEM((2, 2, ny, lanes), F32)))
-            items.append(((name + "_c", level), pltpu.VMEM((2, 4, 8, lanes), F32)))
     for name in ("first_out", "first"):
         items.append((name + "_x", pltpu.VMEM((64, 256), F32)))
         items.append((name + "_y", pltpu.VMEM((48, 256), F32)))
@@ -870,8 +910,8 @@
     items.append(("load", pltpu.SemaphoreType.DMA((24 + len(names),))))
     items.append(("send", pltpu.SemaphoreType.DMA((3, 2, 8))))
     items.append(("recv", pltpu.SemaphoreType.DMA((3, 2, 8))))
-    items.append(("wide_send_sem", pltpu.SemaphoreType.DMA((3, 2, 8))))
-    items.append(("wide_recv_sem", pltpu.SemaphoreType.DMA((3, 2, 8))))
+    items.append(("wide_send_sem", pltpu.SemaphoreType.DMA((3, 2, 14))))
+    items.append(("wide_recv_sem", pltpu.SemaphoreType.DMA((3, 2, 14))))
     items.append(("first_send", pltpu.SemaphoreType.DMA((3,))))
     items.append(("first_recv", pltpu.SemaphoreType.DMA((3,))))
     return items

time: 94.2 us -> 95.7 us (1.016)
  Pallas kernels: 92.2 us -> 93.5 us
    pallas_call x1, Pallas kernels: 92.2 us -> 93.5 us  [local(): pl.pallas_call(functools.partial(kernel, size_x, size_y, names), out_shap...]
where the time goes in v3:
time: 95.7 us; the launch traced here: 95.4 us
  Pallas kernels  93.5 us (98%)
  local copies, waits for them, and re-layouts  1.94 us (2%)
    pallas_call x1, Pallas kernels, local(): pl.pallas_call(functools.partial(kernel, size_x, size_y, names), out_shap...  93.5 us
    unnamed x1, local copies, waits for them, and re-layouts  1.94 us

profile of v3, /device:TPU:25, one launch (start us, length us, event | category | flops | bytes accessed | tf_op | source)
XLA Modules:
  0.0 95.4 jit_solution(5169301111802407143)
XLA Ops:
  0.0 93.5 %shard_map.451 = f32[2,3,192,128]{3,2,1,0:T(8,128)} custom-call(f32[2,3,192,128]{3,2,1,0:T(8,128)} %bitcast.6, f32[192,128]{1,0:T(8,128)} %bitcast.7, s32[192,128]{1,0:T(8,128)} %bitcast.8, f32[2,3]{1,0:T(2,128)} %bitcast.9, bf16[224,32]{1,0:T(8,128)(2,1)} %constant.90.clone.refs_4_, bf16[224,48]{1,0:T(8,128)(2,1)} %constant.91.clone.refs_5_, ...), custom_call_target="tpu_custom_call" | custom-call | tf_op jit(solution)/shard_map/pallas_call | solution.py:934
  93.5 1.9 %copy.51 = f32[2,3,12,16,128]{4,3,2,1,0:T(8,128)} copy(f32[2,3,12,16,128]{4,3,2,1,0:T(8,128)} %bitcast.5) | data formatting | bytes 1179648

commit v4 on v3

--- a/solution.py
+++ b/solution.py
@@ -468,8 +468,8 @@
         begin, length = segment_starts(level)[0][d]
         n = ROWS[level]
         return pltpu.make_async_remote_copy(
-            src_ref=state("wide_send", level).at[slot, :, begin - n : begin - n + length],
-            dst_ref=state("wide_recv", level).at[slot, :, begin : begin + length],
+            src_ref=state("wide_send", level).at[slot, 3 * (begin - n) : 3 * (begin - n + length)],
+            dst_ref=state("wide_recv", level).at[slot, 3 * begin : 3 * (begin + length)],
             send_sem=scratch["wide_send_sem"].at[level, slot, d],
             recv_sem=scratch["wide_recv_sem"].at[level, slot, d],
             device_id=(ix + dx, iy + dy),
@@ -502,6 +502,13 @@
             out.append(part)
             rest = rest - part.astype(F32)
         return out
+
+    def spread_put(level, slot, c, own, others):
+        n = ROWS[level]
+        state("wide_recv", level)[slot, c * n : (c + 1) * n, :] = own
+        for begin, length in segment_starts(level)[0]:
+            row = 3 * (begin - n) + c * length
+            state("wide_send", level)[slot, row : row + length, :] = others[begin - n : begin - n + length]
 
     def spread_values(level, slot, c, value, count):
         n = ROWS[level]
@@ -511,12 +518,18 @@
             hold[k, 0:n, :] = part
             got = dot(const["pk", level][...], hold[k, 0:128, :])
             total = got if total is None else total + got
-        state("wide_send", level)[slot, c] = total
-        state("wide_recv", level)[slot, c, 0:n, :] = value
+        spread_put(level, slot, c, value, total)
 
     def collect(level, slot, c, first_row, count):
-        total = None
-        for part in pieces(state("wide_recv", level)[slot, c], count):
+        total, got, n = None, state("wide_recv", level), ROWS[level]
+        rows = [got[slot, c * n : (c + 1) * n, :]]
+        starts, end = segment_starts(level)
+        for begin, length in starts:
+            row = 3 * begin + c * length
+            rows.append(got[slot, row : row + length, :])
+        if end < gathered(level):
+            rows.append(jnp.zeros((gathered(level) - end, 128), F32))
+        for part in pieces(jnp.concatenate(rows, 0), count):
             got = dot(const["un", level][first_row:, :], part)
             total = got if total is None else total + got
         return total
@@ -641,21 +654,27 @@
                     zhi[slot * kpad : slot * kpad + n, lane] = zh
                     zlo[slot * kpad : slot * kpad + n, lane] = zl
 
-    def across(level, kind, target, n):
+    def across(level, kind, n, put):
         kpad = KPAD[level]
         zhi, zlo = state("zhi", level), state("zlo", level)
         ahi, alo = state(kind + "ahi", level), state(kind + "alo", level)
         for c in range(3):
             span = slice(FIRST_SLOT[c] * kpad, (FIRST_SLOT[c] + 4) * kpad)
             hi, lo = ahi[c, 0:n, :], alo[c, 0:n, :]
-            target[c, 0:n, :] = dot(hi, zhi[span, :]) + dot(hi, zlo[span, :]) + dot(lo, zhi[span, :])
+            put(c, dot(hi, zhi[span, :]) + dot(hi, zlo[span, :]) + dot(lo, zhi[span, :]))
+
+    def into(target, n):
+        def put(c, value):
+            target[c, 0:n, :] = value
+
+        return put
 
     def face_copy(level, slot, d):
         dx, dy = DIRS[d]
-        begin, there, length = message_rows(level)[0][d]
+        _, there, length = message_rows(level)[0][d]
         return pltpu.make_async_remote_copy(
-            src_ref=state("send", level).at[slot, :, begin : begin + length],
-            dst_ref=state("recv", level).at[slot, :, there : there + length],
+            src_ref=state("send", level).at[slot, 3 * there : 3 * (there + length)],
+            dst_ref=state("recv", level).at[slot, 3 * there : 3 * (there + length)],
             send_sem=send_sems.at[level, slot, d],
             recv_sem=recv_sems.at[level, slot, d],
             device_id=(ix + dx, iy + dy),
@@ -663,7 +682,14 @@
         )
 
     def send_faces(level, slot):
-        across(level, "s", state("send", level).at[slot], message_rows(level)[1])
+        spans, sent, _ = message_rows(level)
+
+        def put(c, value):
+            for begin, there, length in spans:
+                row = 3 * there + c * length
+                state("send", level)[slot, row : row + length, :] = value[begin : begin + length]
+
+        across(level, "s", sent, put)
         for d in (4, 5, 6, 7, 0, 1, 2, 3):
 
             @pl.when(exists(*DIRS[d]))
@@ -684,17 +710,17 @@
             def _():
                 face_copy(level, slot, d).wait_recv()
 
-        at = [span[1] for span in message_rows(level)[0]]
-        for c in range(3):
-            t[c, nown : nown + nx, :] += got[slot, c, at[0] : at[0] + nx, :]
-            t[c, 0:py, :] += got[slot, c, at[1] : at[1] + py, :]
-            t[c, corner + 1 : corner + 2, :] += got[slot, c, at[1] + py : at[1] + nx, :]
-            t[c, corner : corner + ny, :] += got[slot, c, at[2] : at[2] + ny, :]
-            t[c, nown : nown + 1, :] += got[slot, c, at[3] : at[3] + 1, :]
+        for c in range(3):
+            at = [3 * there + c * length for _, there, length in message_rows(level)[0]]
+            t[c, nown : nown + nx, :] += got[slot, at[0] : at[0] + nx, :]
+            t[c, 0:py, :] += got[slot, at[1] : at[1] + py, :]
+            t[c, corner + 1 : corner + 2, :] += got[slot, at[1] + py : at[1] + nx, :]
+            t[c, corner : corner + ny, :] += got[slot, at[2] : at[2] + ny, :]
+            t[c, nown : nown + 1, :] += got[slot, at[3] : at[3] + 1, :]
             for x in range(px):
-                t[c, x * py : x * py + 1, :] += got[slot, c, at[3] + 1 + x : at[3] + 2 + x, :]
+                t[c, x * py : x * py + 1, :] += got[slot, at[3] + 1 + x : at[3] + 2 + x, :]
             for k, row in enumerate((corner, 0, corner + 1, nown)):
-                t[c, row : row + 1, :] += got[slot, c, at[4 + k] : at[4 + k] + 1, :]
+                t[c, row : row + 1, :] += got[slot, at[4 + k] : at[4 + k] + 1, :]
 
         for d in range(8):
 
@@ -749,8 +775,7 @@
             hold[1, 0:n, :] = lo
             mat = const["rxy", level][...]
             value = dot(mat, hold[0, 0 : FINE[level], :]) + dot(mat, hold[1, 0 : FINE[level], :])
-            state("wide_recv", level + 1)[slot, c, 0:n_next, :] = value[0:n_next]
-            state("wide_send", level + 1)[slot, c] = value[n_next:]
+            spread_put(level + 1, slot, c, value[0:n_next], value[n_next:])
         spread_start(level + 1, slot)
         spread_wait(level + 1, slot)
         m_next = state("m", level + 1)[...]
@@ -779,14 +804,14 @@
         t = state("t", level)
         for k, (rows_in, rows_out) in enumerate(zip(RINGS[level], RINGS[level][1:])):
             along_z(level, source, rows_in)
-            across(level, "h", t, rows_out)
+            across(level, "h", rows_out, into(t, rows_out))
             update(level, i_first + k, rows_out)
 
     def last(level, i):
         n, t = ROWS[level], state("t", level)
         along_z(level, state("d", level), n)
         send_faces(level, 0)
-        across(level, "", t, n)
+        across(level, "", n, into(t, n))
         add_faces(level, 0, t)
         update(level, i, n)
 
@@ -795,7 +820,7 @@
         start(1)
         near(1, state("d", 1), 1)
         along_z(1, state("x", 1), n)
-        across(1, "", state("t", 1), n)
+        across(1, "", n, into(state("t", 1), n))
         restrict(1, 1)
         start(2)
         near(2, state("d", 2), 1)
@@ -825,7 +850,7 @@
         def _():
             send_faces(0, slot)
 
-        across(0, "", t, n)
+        across(0, "", n, into(t, n))
 
         @pl.when(i != 2)
         def _():
@@ -887,11 +912,11 @@
             for name in ("ahi", "alo"):
                 items.append(((kind + name, level), pltpu.VMEM((3, count, 4 * kpad), BF)))
         if level < 2:
-            items.append((("send", level), pltpu.VMEM((2, 3, sent, lanes), F32)))
-            items.append((("recv", level), pltpu.VMEM((2, 3, got, lanes), F32)))
+            items.append((("send", level), pltpu.VMEM((2, 3 * got, lanes), F32)))
+            items.append((("recv", level), pltpu.VMEM((2, 3 * got, lanes), F32)))
         if level:
-            items.append((("wide_send", level), pltpu.VMEM((2, 3, segment_starts(level)[1] - n, 128), F32)))
-            items.append((("wide_recv", level), pltpu.VMEM((2, 3, gathered(level), 128), F32)))
+            items.append((("wide_send", level), pltpu.VMEM((2, 3 * (segment_starts(level)[1] - n), 128), F32)))
+            items.append((("wide_recv", level), pltpu.VMEM((2, 3 * gathered(level), 128), F32)))
         for name in ("zhi", "zlo"):
             items.append(((name, level), pltpu.VMEM((9 * kpad, lanes), BF)))
     for name in ("first_out", "first"):

time: 95.7 us -> 95.6 us (level)
  no operation moved by 1% of the time
where the time goes in v4:
time: 95.6 us; the launch traced here: 95.3 us
  Pallas kernels  93.4 us (98%)
  local copies, waits for them, and re-layouts  1.94 us (2%)
    pallas_call x1, Pallas kernels, local(): pl.pallas_call(functools.partial(kernel, size_x, size_y, names), out_shap...  93.4 us
    unnamed x1, local copies, waits for them, and re-layouts  1.94 us

profile of v4, /device:TPU:25, one launch (start us, length us, event | category | flops | bytes accessed | tf_op | source)
XLA Modules:
  0.0 95.3 jit_solution(1461007454736370684)
XLA Ops:
  0.0 93.4 %shard_map.451 = f32[2,3,192,128]{3,2,1,0:T(8,128)} custom-call(f32[2,3,192,128]{3,2,1,0:T(8,128)} %bitcast.6, f32[192,128]{1,0:T(8,128)} %bitcast.7, s32[192,128]{1,0:T(8,128)} %bitcast.8, f32[2,3]{1,0:T(2,128)} %bitcast.9, bf16[224,32]{1,0:T(8,128)(2,1)} %constant.90.clone.refs_4_, bf16[224,48]{1,0:T(8,128)(2,1)} %constant.91.clone.refs_5_, ...), custom_call_target="tpu_custom_call" | custom-call | tf_op jit(solution)/shard_map/pallas_call | solution.py:959
  93.4 1.9 %copy.51 = f32[2,3,12,16,128]{4,3,2,1,0:T(8,128)} copy(f32[2,3,12,16,128]{4,3,2,1,0:T(8,128)} %bitcast.5) | data formatting | bytes 1179648

commit v5 on v2

--- a/solution.py
+++ b/solution.py
@@ -898,7 +898,7 @@
             out_specs=any_spec,
             scratch_shapes=[item for _, item in scratch_list(names, shapes)],
             compiler_params=pltpu.CompilerParams(
-                collective_id=0, has_side_effects=True, vmem_limit_bytes=60 * 1024 * 1024
+                collective_id=0, has_side_effects=True, vmem_limit_bytes=40 * 1024 * 1024
             ),
         )(
             modes.reshape(VECS, 3, own, 128),

time: 94.2 us -> 140 us (1.49); the launches traced: 94.1 us -> 137 us
  local copies, waits for them, and re-layouts: 1.94 us -> 40.1 us
  Pallas kernels: 92.2 us -> 97.2 us
    unnamed x1 -> x99, local copies, waits for them, and re-layouts: 1.94 us -> 40.1 us
    pallas_call x1, Pallas kernels: 92.2 us -> 97.2 us  [local(): pl.pallas_call(functools.partial(kernel, size_x, size_y, names), out_shap...]
where the time goes in v5:
time: 140 us; the launch traced here: 137 us
  Pallas kernels  97.2 us (69%)
  local copies, waits for them, and re-layouts  40.1 us (29%)
    pallas_call x1, Pallas kernels, local(): pl.pallas_call(functools.partial(kernel, size_x, size_y, names), out_shap...  97.2 us
    unnamed x99, local copies, waits for them, and re-layouts  40.1 us

profile of v5, /device:TPU:25, one launch (start us, length us, event | category | flops | bytes accessed | tf_op | source)
XLA Modules:
  0.0 137.4 jit_solution(10663207966709380595)
XLA Ops:
  0.0 0.0 copy-start.17
  0.0 0.0 copy-start.37
  0.0 0.9 copy-done.17
  0.9 0.0 copy-done.37
  0.9 0.0 copy-start
  0.9 1.1 copy-done
  2.0 0.0 copy-start.1
  2.0 0.9 copy-done.1
  2.9 0.0 copy-start.2
  2.9 0.9 copy-done.2
  3.9 0.0 copy-start.3
  3.9 0.9 copy-done.3
  4.8 0.0 copy-start.4
  4.8 0.9 copy-done.4
  5.7 0.0 copy-start.5
  5.7 0.9 copy-done.5
  6.7 0.9 copy-done.6
  7.6 0.0 copy-start.7
  7.6 0.9 copy-done.7
  8.5 0.0 copy-start.8
  8.5 0.9 copy-done.8
  9.4 0.0 copy-start.9
  9.4 0.9 copy-done.9
  10.4 0.0 copy-start.10
  10.4 0.9 copy-done.10
  11.3 0.0 copy-start.11
  11.3 0.9 copy-done.11
  12.2 0.9 copy-done.12
  13.1 0.9 copy-done.13
  14.0 0.9 copy-done.14
  14.8 0.9 copy-done.15
  15.7 0.9 copy-done.16
  16.6 0.8 copy-done.18
  17.5 0.8 copy-done.19
  18.3 0.8 copy-done.20
  19.1 0.8 copy-done.21
  20.0 0.8 copy-done.22
  20.8 0.8 copy-done.23
  21.6 0.8 copy-done.24
  22.4 0.8 copy-done.25
  23.2 0.8 copy-done.26
  24.0 0.8 copy-done.27
  24.8 0.8 copy-done.28
  25.6 0.8 copy-done.29
  26.4 0.8 copy-done.30
  27.1 0.8 copy-done.31
  27.9 0.8 copy-done.32
  28.6 0.8 copy-done.33
  29.4 0.8 copy-done.34
  30.2 0.8 copy-done.35
  30.9 0.8 copy-done.36
  31.7 0.7 copy-done.38
  32.4 0.7 copy-done.39
  33.1 0.7 copy-done.40
  33.8 0.7 copy-done.41
  34.5 0.7 copy-done.42
  35.2 0.7 copy-done.43
  35.9 0.7 copy-done.44
  36.6 0.7 copy-done.45
  37.3 0.7 copy-done.46
  38.0 0.7 copy-done.47
  38.7 0.7 copy-done.48
  39.4 97.2 %shard_map.451 = f32[2,3,192,128]{3,2,1,0:T(8,128)S(1)} custom-call(f32[2,3,192,128]{3,2,1,0:T(8,128)S(1)} %bitcast.6, f32[192,128]{1,0:T(8,128)S(1)} %bitcast.7, s32[192,128]{1,0:T(8,128)S(1)} %bitcast.8, f32[2,3]{1,0:T(2,128)S(1)} %bitcast.9, bf16[224,32]{1,0:T(8,128)(2,1)S(1)} %copy-done.24, bf16[224,48]{1,0:T(8,128)(2,1)S(1)} %copy-done.23, ...), custom_call_target="tpu_custom_call" | custom-call | tf_op jit(solution)/shard_map/pallas_call | solution.py:894
  136.6 0.8 copy.51
  (36 shorter events, 0.1 us)
Async XLA Ops:
  0.0 0.9 copy-start.17
  0.0 0.9 copy-start.37
  0.9 1.1 copy-start
  2.0 0.9 copy-start.1
  2.9 0.9 copy-start.2
  3.9 0.9 copy-start.3
  4.8 0.9 copy-start.4
  5.7 0.9 copy-start.5
  6.7 0.9 copy-start.6
  7.6 0.9 copy-start.7
  8.5 0.9 copy-start.8
  9.4 0.9 copy-start.9
  10.4 0.9 copy-start.10
  11.3 0.9 copy-start.11
  12.2 0.9 copy-start.12
  13.1 0.9 copy-start.13
  14.0 0.9 copy-start.14
  14.8 0.9 copy-start.15
  15.7 0.9 copy-start.16
  16.6 0.8 copy-start.18
  17.5 0.8 copy-start.19
  18.3 0.8 copy-start.20
  19.1 0.8 copy-start.21
  20.0 0.8 copy-start.22
  20.8 0.8 copy-start.23
  21.6 0.8 copy-start.24
  22.4 0.8 copy-start.25
  23.2 0.8 copy-start.26
  24.0 0.8 copy-start.27
  24.8 0.8 copy-start.28
  25.6 0.8 copy-start.29
  26.4 0.8 copy-start.30
  27.1 0.8 copy-start.31
  27.9 0.8 copy-start.32
  28.6 0.8 copy-start.33
  29.4 0.8 copy-start.34
  30.2 0.8 copy-start.35
  30.9 0.8 copy-start.36
  31.7 0.7 copy-start.38
  32.4 0.7 copy-start.39
  33.1 0.7 copy-start.40
  33.8 0.7 copy-start.41
  34.5 0.7 copy-start.42
  35.2 0.7 copy-start.43
  35.9 0.7 copy-start.44
  36.6 0.7 copy-start.45
  37.3 0.7 copy-start.46
  38.0 0.7 copy-start.47
  38.7 0.7 copy-start.48
